TPU v7x, 256 devices: a whole 4x4x8 slice. The times are simulated.
256 devices in a mesh: grp: 4 (over x), wide: 64 (over y, z, core).
Axes of the slice: x: 4, y: 4, z: 8, core: 2. Of those that a mesh axis runs over, the one named last changes fastest.
Arguments:
- leaf_entries: float32 [4, 128, 512, 512], P('grp', 'wide'), may hold values from -8 to 14, as said below
- leaf_tiles: int32 [4, 128], P('grp', 'wide'), may hold values from 1 to 3
- leaf_map: int32 [4, 128, 3], P('grp', 'wide'), may hold values from 0 to 7, as said below
- mid_entries: float32 [4, 64, 1024, 1024], P('grp', 'wide'), may hold values from -8 to 14, as said below
- mid_tiles: int32 [4, 64], P('grp', 'wide'), may hold values from 3 to 7, as said below
- mid_map: int32 [4, 64, 7], P('grp', 'wide'), may hold values from 0 to 55, as said below
- root_panel_entries: float32 [4, 7680, 512], P('grp', 'wide'), may hold values from -8 to 14, as said below
- root_update_entries: float32 [4, 64, 896, 896], P('grp', 'wide'), may hold values from -1 to 5, as said below
Outputs:
- root_panel: float32 [4, 7680, 512], P('grp', 'wide')
- top_update: float32 [64, 896, 896], P('wide', 'grp')
Inputs may be any that keep to these rules, and one draw needn't show every extreme that they name: `mid_tiles`: each group has a middle front with 7 live update tiles. `leaf_map`: the 3 entries of one leaf are distinct and less than 1 + mid_tiles of its middle front. `mid_map`: entry a of a middle front lies in the block (s + a) mod 8 of 7 consecutive tiles, s a multiple of 1 chosen for each front; so the live tiles of one middle update that land in one block of step four number at most 1, and in every draw some middle update sends exactly 1 to one block. `leaf_entries`: each leaf front is symmetric positive definite. `mid_entries`: each middle front is symmetric positive definite. `root_panel_entries`: the first 512 rows form a symmetric positive definite block. `root_update_entries`: the assembled square of step four before the additions is symmetric.
All inputs are finite; a program needn't handle non-finite values.
Results may differ from a plain program's by a relative error of at most 0.0003.
Values sent between devices are 32-bit elements; how exact they have to be, the bound alone decides.
No kernel may reach another device: no remote copies, remote signals or barrier semaphores. Data moves between devices by JAX's collectives and lax.ppermute only.
A program may use at most 128 MiB of HBM per device.

v0:
```python
import jax
import jax.numpy as jnp
from jax import lax
from jax.experimental import pallas as pl
from jax.experimental.pallas import tpu as pltpu
from jax.sharding import Mesh, PartitionSpec as P


TILE = 128
UL = 3
UM = 7
K = 4
BLK = 16
SLOT = 136
PANEL = 120
CHUNK = 112
MIXED = PANEL + CHUNK
SIDE = 896
HI = lax.Precision.HIGHEST
F32 = jnp.float32
COST = 1 << 31
WIDE = ("y", "h", "l", "c")


def dot(lhs, rhs, contract):
    return lax.dot_general(
        lhs, rhs, (contract, ((), ())), precision=HI, preferred_element_type=F32
    )


def factor_rows(panels):
    for block in range(TILE // BLK):
        low = block * BLK
        high = low + BLK
        work = []
        for ref, row, col, tiles in panels:
            rows = [
                ref[pl.ds(row + low, BLK), pl.ds(col + t * TILE, TILE)] for t in range(tiles)
            ]
            cols = [
                jnp.broadcast_to(rows[0][:, low + m : low + m + 1], (BLK, TILE))
                for m in range(BLK)
            ]
            work.append((rows, cols))
        for step in range(BLK):
            for (ref, row, col, tiles), (rows, cols) in zip(panels, work):
                inverse = lax.rsqrt(cols[step][step : step + 1, :])
                lower = cols[step] * inverse
                for t in range(tiles):
                    upper = rows[t][step : step + 1, :] * inverse
                    ref[pl.ds(row + low + step, 1), pl.ds(col + t * TILE, TILE)] = upper
                    if step + 1 < BLK:
                        rows[t] = rows[t] - lower * upper
                for m in range(step + 1, BLK):
                    cols[m] = cols[m] - lower * lower[m : m + 1, :]
        if high < TILE:
            for ref, row, col, tiles in panels:
                wide = pl.ds(col, tiles * TILE)
                strip = ref[pl.ds(row + low, BLK), wide]
                product = dot(strip[:, :TILE], strip, ((0,), (0,)))
                rest = pl.ds(row + high, TILE - high)
                ref[rest, wide] = ref[rest, wide] - product[high:]


def leaf_kernel(leaf_ref, out_ref, top):
    for i in range(2):
        top[i * TILE : (i + 1) * TILE, :] = leaf_ref[i, :TILE, :]
    factor_rows([(top, i * TILE, 0, UL + 1) for i in range(2)])
    for i in range(2):
        coupling = top[i * TILE : (i + 1) * TILE, TILE:]
        out_ref[i] = leaf_ref[i, TILE:, TILE:] - dot(coupling, coupling, ((0,), (0,)))


def leaves(leaf):
    return pl.pallas_call(
        leaf_kernel,
        out_shape=jax.ShapeDtypeStruct((2, UL * TILE, UL * TILE), F32),
        scratch_shapes=[pltpu.VMEM((2 * TILE, (UL + 1) * TILE), F32)],
        cost_estimate=pl.CostEstimate(flops=COST, bytes_accessed=3 << 20, transcendentals=0),
        name="leaves",
    )(leaf)


def middle_kernel(
    leaf_live, leaf_map, mid_live, mid_map, leaf_ref, mid_hbm, chunk_hbm, block_hbm, out_hbm,
    mid, update, spots, load_sem, send_sem, spot_sem,
):
    head = pltpu.make_async_copy(mid_hbm.at[:TILE], mid.at[:TILE], load_sem.at[0])
    rest = pltpu.make_async_copy(mid_hbm.at[TILE:], mid.at[TILE:], load_sem.at[1])
    head.start()
    rest.start()

    def assemble(in_head):
        for i in range(2):
            live = leaf_live[i]
            for a in range(UL):
                to_row = leaf_map[i * UL + a]
                row = pl.multiple_of(to_row * TILE, TILE)
                wanted = (to_row == 0) if in_head else (to_row > 0)
                for b in range(UL):
                    col = pl.multiple_of(leaf_map[i * UL + b] * TILE, TILE)

                    @pl.when(wanted & (a < live) & (b < live))
                    def _():
                        mid[pl.ds(row, TILE), pl.ds(col, TILE)] = (
                            mid[pl.ds(row, TILE), pl.ds(col, TILE)]
                            + leaf_ref[i, a * TILE : (a + 1) * TILE, b * TILE : (b + 1) * TILE]
                        )

    head.wait()
    assemble(True)
    factor_rows([(mid, 0, 0, UM + 1)])
    rest.wait()
    assemble(False)
    live = mid_live[0]
    spots[...] = jnp.zeros((64, SLOT - TILE, TILE), F32)
    copies = []
    for a in range(UM):
        update[a * TILE : (a + 1) * TILE, :] = mid[(a + 1) * TILE : (a + 2) * TILE, TILE:] - dot(
            mid[:TILE, (a + 1) * TILE : (a + 2) * TILE], mid[:TILE, TILE:], ((0,), (0,))
        )
        to_row = mid_map[a]
        for b in range(UM):
            to_col = mid_map[b]
            slot = (to_row // 7) * 8 + to_col // 7
            spot = (to_row % 7) * 7 + to_col % 7 + 1
            spot = jnp.where((a < live) & (b < live), spot, 0)
            spots[slot] = jnp.full((SLOT - TILE, TILE), spot.astype(F32), F32)
            copy = pltpu.make_async_copy(
                update.at[a * TILE : (a + 1) * TILE, b * TILE : (b + 1) * TILE],
                out_hbm.at[slot, :TILE, :],
                send_sem.at[a * UM + b],
            )
            copy.start()
            copies.append(copy)
    mark = pltpu.make_async_copy(spots, out_hbm.at[:, TILE:, :], spot_sem)
    mark.start()
    for copy in copies:
        copy.wait()
    mark.wait()


def middles(leaf_live, leaf_map, mid_live, mid_map, leaf, mid, chunk, block):
    smem = pl.BlockSpec(memory_space=pltpu.SMEM)
    vmem = pl.BlockSpec(memory_space=pltpu.VMEM)
    hbm = pl.BlockSpec(memory_space=pl.ANY)
    return pl.pallas_call(
        middle_kernel,
        out_shape=jax.ShapeDtypeStruct((64, SLOT, TILE), F32),
        in_specs=[smem, smem, smem, smem, vmem, hbm, hbm, hbm],
        out_specs=hbm,
        scratch_shapes=[
            pltpu.VMEM((1024, 1024), F32),
            pltpu.VMEM((SIDE, SIDE), F32),
            pltpu.VMEM((64, SLOT - TILE, TILE), F32),
            pltpu.SemaphoreType.DMA((2,)),
            pltpu.SemaphoreType.DMA((UM * UM,)),
            pltpu.SemaphoreType.DMA,
        ],
        cost_estimate=pl.CostEstimate(flops=COST, bytes_accessed=9 << 20, transcendentals=0),
        name="middles",
    )(leaf_live, leaf_map, mid_live, mid_map, leaf, mid, chunk, block)


def pivot_kernel(place_at, pieces_ref, inverse_ref, work, panel):
    width = K * TILE
    eye = (
        lax.broadcasted_iota(jnp.int32, (width, width), 0)
        == lax.broadcasted_iota(jnp.int32, (width, width), 1)
    ).astype(F32)
    work[:, width:] = eye
    for piece in range(8):
        at = place_at[piece]
        part = pieces_ref[piece * MIXED + CHUNK : (piece + 1) * MIXED, :]

        @pl.when(at < K)
        def _():
            work[pl.ds(pl.multiple_of(at * PANEL, 8), PANEL), :width] = part

        @pl.when(at == K)
        def _():
            work[K * PANEL : width, :width] = part[: width - K * PANEL]

    def step(k, carry):
        base = pl.multiple_of(k * TILE, TILE)
        cols = pl.ds(base, (K + 1) * TILE)
        panel[...] = work[pl.ds(base, TILE), cols]
        factor_rows([(panel, 0, 0, K + 1)])
        work[pl.ds(base, TILE), cols] = panel[...]
        for m in range(1, K):

            @pl.when(m > k)
            def _():
                rows = slice(m * TILE, (m + 1) * TILE)
                work[rows, cols] = work[rows, cols] - dot(
                    work[pl.ds(base, TILE), rows], panel[...], ((0,), (0,))
                )

        return carry

    lax.fori_loop(0, K, step, 0)
    inverse_ref[...] = work[:, width:]


def pivots(place_at, pieces):
    width = K * TILE
    vmem = pl.BlockSpec(memory_space=pltpu.VMEM)
    return pl.pallas_call(
        pivot_kernel,
        out_shape=jax.ShapeDtypeStruct((width, width), F32),
        in_specs=[pl.BlockSpec(memory_space=pltpu.SMEM), vmem],
        out_specs=vmem,
        scratch_shapes=[
            pltpu.VMEM((width, 2 * width), F32),
            pltpu.VMEM((TILE, (K + 1) * TILE), F32),
        ],
        cost_estimate=pl.CostEstimate(flops=2 * COST, bytes_accessed=2 << 20, transcendentals=0),
        name="pivots",
    )(place_at, pieces)


def split(value):
    high = value.astype(jnp.bfloat16)
    return high, (value - high.astype(F32)).astype(jnp.bfloat16)


def update_kernel(
    first, place_at, quarter_at, pieces_ref, own_ref, inverse_ref, entry_ref, *rest
):
    quarter_refs, (panel_ref, out_ref, raw, high, low) = rest[:4], rest[4:]
    width = K * TILE
    inverse = inverse_ref[...]
    rows_at = first[0] + lax.broadcasted_iota(jnp.int32, (PANEL, width), 0)
    column = lax.broadcasted_iota(jnp.int32, (PANEL, width), 1)
    live = (column <= rows_at) | (rows_at >= width)
    panel_ref[...] = jnp.where(live, dot(own_ref[...], inverse, ((1,), (1,))), 0.0)
    for piece in range(8):
        raw[0, pl.ds(pl.multiple_of(place_at[piece] * CHUNK, 8), CHUNK), :] = pieces_ref[
            piece * MIXED : piece * MIXED + CHUNK, :
        ]
    for piece, ref in enumerate(quarter_refs):
        at = pl.multiple_of(quarter_at[piece] * 2 * CHUNK, 8)
        raw[1, pl.ds(at, 2 * CHUNK), :] = ref[...]
    for side in range(2):
        high[side], low[side] = split(dot(raw[side], inverse, ((1,), (1,))))

    def product(lhs, rhs):
        return lax.dot_general(
            lhs, rhs, (((1,), (1,)), ((), ())), preferred_element_type=F32
        )

    for t in range(7):
        at = slice(t * TILE, (t + 1) * TILE)
        out_ref[at, :] = entry_ref[at, :] - (
            product(high[0, at, :], high[1])
            + (product(high[0, at, :], low[1]) + product(low[0, at, :], high[1]))
        )


def updates(first, place_at, quarter_at, pieces, own, inverse, entries, quarters):
    vmem = pl.BlockSpec(memory_space=pltpu.VMEM)
    return pl.pallas_call(
        update_kernel,
        out_shape=(
            jax.ShapeDtypeStruct((PANEL, K * TILE), F32),
            jax.ShapeDtypeStruct((SIDE, SIDE), F32),
        ),
        in_specs=[pl.BlockSpec(memory_space=pltpu.SMEM)] * 3 + [vmem] * 8,
        out_specs=(vmem, vmem),
        scratch_shapes=[
            pltpu.VMEM((2, SIDE, K * TILE), F32),
            pltpu.VMEM((2, SIDE, K * TILE), jnp.bfloat16),
            pltpu.VMEM((2, SIDE, K * TILE), jnp.bfloat16),
        ],
        cost_estimate=pl.CostEstimate(flops=COST, bytes_accessed=12 << 20, transcendentals=0),
        name="updates",
    )(first, place_at, quarter_at, pieces, own, inverse, entries, *quarters)


def place_kernel(incoming_hbm, base_ref, out_ref, incoming, spots, sem, spot_sem):
    parts = 4
    count = 64 // parts
    mark = pltpu.make_async_copy(incoming_hbm.at[:, TILE, :], spots, spot_sem)
    mark.start()
    copies = []
    for part in range(parts):
        at = pl.ds(part * count, count)
        copy = pltpu.make_async_copy(
            incoming_hbm.at[at, :TILE, :], incoming.at[at], sem.at[part]
        )
        copy.start()
        copies.append(copy)
    out_ref[...] = base_ref[...]
    mark.wait()
    for part, copy in enumerate(copies):
        copy.wait()

        def body(s, carry):
            spot = spots[s, 0].astype(jnp.int32)

            @pl.when(spot > 0)
            def _():
                row = pl.multiple_of(((spot - 1) // 7) * TILE, TILE)
                col = pl.multiple_of(((spot - 1) % 7) * TILE, TILE)
                out_ref[pl.ds(row, TILE), pl.ds(col, TILE)] = (
                    out_ref[pl.ds(row, TILE), pl.ds(col, TILE)] + incoming[s]
                )

            return carry

        lax.fori_loop(part * count, (part + 1) * count, body, 0)


def place(incoming, base):
    vmem = pl.BlockSpec(memory_space=pltpu.VMEM)
    return pl.pallas_call(
        place_kernel,
        out_shape=jax.ShapeDtypeStruct((SIDE, SIDE), F32),
        in_specs=[pl.BlockSpec(memory_space=pl.ANY), vmem],
        out_specs=vmem,
        scratch_shapes=[
            pltpu.VMEM((64, TILE, TILE), F32),
            pltpu.SMEM((64, TILE), F32),
            pltpu.SemaphoreType.DMA((4,)),
            pltpu.SemaphoreType.DMA,
        ],
        cost_estimate=pl.CostEstimate(flops=COST, bytes_accessed=12 << 20, transcendentals=0),
        name="place",
    )(incoming, base)


def chunk_source(d):
    return divmod(K * TILE + CHUNK * d, PANEL)


def rechunk_pairs():
    first, second, third = [], [], []
    taken = set()
    for d in range(64):
        source, offset = chunk_source(d)
        if source in taken:
            third.append((source, d))
        else:
            taken.add(source)
            first.append((source, d))
        if offset + CHUNK > PANEL:
            second.append((source + 1, d))
    return first, second, third


def across(pairs):
    return [(a * 8 + q, b * 8 + q) for a, b in pairs for q in range(8)]


def program(
    leaf_entries,
    leaf_tiles,
    leaf_map,
    mid_entries,
    mid_tiles,
    mid_map,
    root_panel_entries,
    root_update_entries,
):
    position = lax.axis_index(WIDE)
    row = position // 8
    panel = root_panel_entries[0]
    first, second, third = rechunk_pairs()
    head = lax.ppermute(panel, WIDE, first)
    tail = lax.ppermute(panel, WIDE, second)
    extra = lax.ppermute(panel[CHUNK:], WIDE, third)
    spread = [lax.ppermute(panel, WIDE, across([(0, b)])) for b in (1, 2, 6)]
    leaf_updates = leaves(leaf_entries[0])
    joined = jnp.concatenate([head[:CHUNK], head[CHUNK:] + extra, tail], axis=0)
    offset = (K * TILE + CHUNK * position) % PANEL
    chunk = lax.dynamic_slice_in_dim(joined, offset, CHUNK, 0)
    block = jnp.where(row == 0, panel, 0.0) + (spread[0] + spread[1] + spread[2])
    straight = lax.ppermute(
        chunk, WIDE, [(p * 8 + q, q * 8 + p) for p in range(8) for q in range(8)]
    )
    crossed = lax.ppermute(
        chunk, WIDE, [(p * 8 + q, (q ^ 1) * 8 + p) for p in range(8) for q in range(8)]
    )
    last = lax.ppermute(block, WIDE, across([(1, 3), (2, 4), (6, 7), (0, 5)]))
    outgoing = middles(
        leaf_tiles[0],
        leaf_map[0].reshape(-1),
        mid_tiles[0],
        mid_map[0, 0],
        leaf_updates,
        mid_entries[0, 0],
        chunk,
        block,
    )
    pair = jnp.where(
        row % 2 == 0,
        jnp.concatenate([straight, crossed], axis=0),
        jnp.concatenate([crossed, straight], axis=0),
    )
    mixed = jnp.concatenate([chunk, block + last], axis=0)
    parts = [mixed] + [
        lax.ppermute(mixed, WIDE, [(d, d ^ (2 * k)) for d in range(64)]) for k in (1, 2, 3)
    ]
    quarters = [pair] + [
        lax.ppermute(pair, WIDE, [(d, d ^ (16 * k)) for d in range(64)]) for k in (1, 2, 3)
    ]
    incoming = lax.all_to_all(outgoing, WIDE, 0, 0, tiled=True)
    pieces = lax.all_gather(jnp.concatenate(parts, axis=0), "c", axis=0, tiled=True)
    order = jnp.arange(4, dtype=jnp.int32)
    line = lax.axis_index("l") ^ order
    place_at = jnp.concatenate([2 * line, 2 * line + 1])
    inverse = pivots(place_at, pieces)
    root_panel, base = updates(
        (position * PANEL).reshape(1),
        place_at,
        lax.axis_index("y") ^ order,
        pieces,
        panel,
        inverse,
        root_update_entries[0, 0],
        quarters,
    )
    total = place(incoming, base)
    top_part = lax.psum_scatter(total, "grp", scatter_dimension=0, tiled=True)
    return (root_panel[None], top_part[None])


def solution(mesh):
    fine = Mesh(mesh.devices.reshape(4, 4, 2, 4, 2), ("grp",) + WIDE)
    placed = (
        P("grp", WIDE, None, None),
        P("grp", WIDE),
        P("grp", WIDE, None),
        P("grp", WIDE, None, None),
        P("grp", WIDE),
        P("grp", WIDE, None),
        P("grp", WIDE, None),
        P("grp", WIDE, None, None),
    )
    return jax.shard_map(
        program,
        mesh=fine,
        in_specs=placed,
        out_specs=(P("grp", WIDE, None), P(WIDE, "grp", None)),
        check_vma=False,
    )
```

profile of v0, /device:TPU:1, one launch (start us, length us, event | category | flops | bytes accessed | tf_op | source)
XLA Modules:
  0.0 350.7 jit_solution(4102662380325179768)
XLA Ops:
  7.2 5.5 %collective-permute-start.5 = (f32[120,512]{1,0:T(8,128)}, f32[120,512]{1,0:T(8,128)S(1)}, u32[]{:S(2)}, u32[]{:S(2)}) collective-permute-start(f32[120,512]{1,0:T(8,128)} %bitcast.16), channel_id=1, source_target_pairs={{0,48},{1,49},{2,50},{3,51},{4,52},{5,53},{6,54},{7,55},{64,112},{... | collective-permute-start | bytes 737288 | tf_op jit(solution)/shard_map/ppermute | solution.py:372
  12.6 1.3 collective-permute-start.4
  14.0 4.2 %collective-permute-start.3 = (f32[120,512]{1,0:T(8,128)}, f32[120,512]{1,0:T(8,128)S(1)}, u32[]{:S(2)}, u32[]{:S(2)}) collective-permute-start(f32[120,512]{1,0:T(8,128)} %bitcast.18), channel_id=1, source_target_pairs={{0,8},{1,9},{2,10},{3,11},{4,12},{5,13},{6,14},{7,15},{64,72},{65,... | collective-permute-start | bytes 737288 | tf_op jit(solution)/shard_map/ppermute | solution.py:372
  18.2 1.3 collective-permute-start
  19.5 0.7 slice_bitcast_fusion
  20.2 0.7 collective-permute-start.1
  20.9 9.1 %leaves.1.leaf_ref = f32[2,384,384]{2,1,0:T(8,128)} custom-call(f32[2,512,512]{2,1,0:T(8,128)} %bitcast.24), custom_call_target="tpu_custom_call" | custom-call | flops 2147483648 | bytes 3145728 | tf_op jit(solution)/shard_map/leaves/pallas_call | solution.py:75
  31.2 5.8 %collective-permute-done = f32[120,512]{1,0:T(8,128)S(1)} collective-permute-done((f32[120,512]{1,0:T(8,128)}, f32[120,512]{1,0:T(8,128)S(1)}, u32[]{:S(2)}, u32[]{:S(2)}) %collective-permute-start) | collective-permute-done | bytes 245792 | tf_op jit(solution)/shard_map/ppermute | solution.py:369
  37.0 1.3 collective-permute-start.2
  38.4 0.8 add_add_fusion.block_hbm
  39.2 9.4 %collective-permute-done.2 = f32[120,512]{1,0:T(8,128)S(1)} collective-permute-done((f32[120,512]{1,0:T(8,128)S(1)}, f32[120,512]{1,0:T(8,128)S(1)}, u32[]{:S(2)}, u32[]{:S(2)}) %collective-permute-start.2) | collective-permute-done | bytes 245792 | tf_op jit(solution)/shard_map/ppermute | solution.py:370
  48.6 0.8 constant_dynamic-update-slice_fusion.4
  49.4 12.0 %middles.1 = f32[64,136,128]{2,1,0:T(8,128)} custom-call(s32[2]{0:T(128)} %bitcast.22, s32[6]{0:T(128)} %reshape_squeeze.3.leaf_map, s32[1]{0:T(128)} %bitcast.13.mid_live, s32[7]{0:T(128)} %bitcast.23, f32[2,384,384]{2,1,0:T(8,128)} %leaves.1.leaf_ref, f32[1024,1024]{1,0:T(8,128)} %bitcast.14, f32[112,512]{1,0:T(8,128)} %get-tuple-element.9.chunk_hbm, ...), custom_call_target="tpu_custom_call" | custom-call | flops 2147483648 | bytes 9437184 | tf_op jit(solution)/shard_map/middles/pallas_call | solution.py:147
  61.5 5.9 %all-to-all-start = ((f32[64,136,128]{2,1,0:T(8,128)}), f32[64,136,128]{2,1,0:T(8,128)}, u32[]{:S(2)}, u32[]{:S(2)}) async-start(f32[64,136,128]{2,1,0:T(8,128)} %middles.1), calls=%async_computation | async-start | bytes 8912896 | tf_op jit(solution)/shard_map/all_to_all | solution.py:407
  67.5 9.7 %collective-permute-start.6 = (f32[120,512]{1,0:T(8,128)S(1)}, f32[120,512]{1,0:T(8,128)S(1)}, u32[]{:S(2)}, u32[]{:S(2)}) collective-permute-start(f32[120,512]{1,0:T(8,128)S(1)} %copy-done.1), channel_id=1, source_target_pairs={{8,24},{9,25},{10,26},{11,27},{12,28},{13,29},{14,30},{15,31},{16,... | collective-permute-start | bytes 737288 | tf_op jit(solution)/shard_map/ppermute | solution.py:384
  77.2 90.5 %collective-permute-done.6 = f32[120,512]{1,0:T(8,128)S(1)} collective-permute-done((f32[120,512]{1,0:T(8,128)S(1)}, f32[120,512]{1,0:T(8,128)S(1)}, u32[]{:S(2)}, u32[]{:S(2)}) %collective-permute-start.6) | collective-permute-done | bytes 245792 | tf_op jit(solution)/shard_map/ppermute | solution.py:384
  167.8 6.8 %collective-permute-start.7 = (f32[232,512]{1,0:T(8,128)S(1)}, f32[232,512]{1,0:T(8,128)S(1)}, u32[]{:S(2)}, u32[]{:S(2)}) collective-permute-start(f32[232,512]{1,0:T(8,128)S(1)} %pad_maximum_fusion), channel_id=1, source_target_pairs={{0,2},{1,3},{2,0},{3,1},{4,6},{5,7},{6,4},{7,5},{8,10},{9,11},{10,... | collective-permute-start | bytes 1425416 | tf_op jit(solution)/shard_map/ppermute | solution.py:402
  174.7 1.3 collective-permute-start.8
  176.0 1.1 collective-permute-start.9
  177.0 17.3 %collective-permute-done.7 = f32[232,512]{1,0:T(8,128)S(1)} collective-permute-done((f32[232,512]{1,0:T(8,128)S(1)}, f32[232,512]{1,0:T(8,128)S(1)}, u32[]{:S(2)}, u32[]{:S(2)}) %collective-permute-start.7) | collective-permute-done | bytes 475168 | tf_op jit(solution)/shard_map/ppermute | solution.py:402
  194.4 13.5 %collective-permute-done.9 = f32[232,512]{1,0:T(8,128)S(1)} collective-permute-done((f32[232,512]{1,0:T(8,128)S(1)}, f32[232,512]{1,0:T(8,128)S(1)}, u32[]{:S(2)}, u32[]{:S(2)}) %collective-permute-start.9) | collective-permute-done | bytes 475168 | tf_op jit(solution)/shard_map/ppermute | solution.py:402
  208.0 1.2 copy-done
  209.3 1.9 collective-permute-start.10
  211.2 1.9 collective-permute-start.11
  213.6 9.2 %collective-permute-done.10 = f32[112,512]{1,0:T(8,128)S(1)} collective-permute-done((f32[112,512]{1,0:T(8,128)S(1)}, f32[112,512]{1,0:T(8,128)S(1)}, u32[]{:S(2)}, u32[]{:S(2)}) %collective-permute-start.10) | collective-permute-done | bytes 229408 | tf_op jit(solution)/shard_map/ppermute | solution.py:378
  222.9 17.0 %collective-permute-start.14 = (f32[224,512]{1,0:T(8,128)S(1)}, f32[224,512]{1,0:T(8,128)S(1)}, u32[]{:S(2)}, u32[]{:S(2)}) collective-permute-start(f32[224,512]{1,0:T(8,128)S(1)} %maximum_select_fusion.rest_0_), channel_id=1, source_target_pairs={{0,48},{1,49},{2,50},{3,51},{4,52},{5,53},{6,54},{7,55},{8,56},{9,... | collective-permute-start | bytes 1376264 | tf_op jit(solution)/shard_map/ppermute | solution.py:405
  239.9 7.1 %collective-permute-start.13 = (f32[224,512]{1,0:T(8,128)S(1)}, f32[224,512]{1,0:T(8,128)S(1)}, u32[]{:S(2)}, u32[]{:S(2)}) collective-permute-start(f32[224,512]{1,0:T(8,128)S(1)} %maximum_select_fusion.rest_0_), channel_id=1, source_target_pairs={{0,32},{1,33},{2,34},{3,35},{4,36},{5,37},{6,38},{7,39},{8,40},{9,... | collective-permute-start | bytes 1376264 | tf_op jit(solution)/shard_map/ppermute | solution.py:405
  247.6 25.5 %pivots.1.inverse_ref = f32[512,512]{1,0:T(8,128)} custom-call(s32[8]{0:T(128)} %pad_add_fusion.place_at, f32[1856,512]{1,0:T(8,128)} %all-gather.2.cloned.1.call-done.pieces_ref), custom_call_target="tpu_custom_call" | custom-call | flops 4294967296 | bytes 2097152 | tf_op jit(solution)/shard_map/pivots/pallas_call | solution.py:208
  273.2 0.7 copy-done.5
  274.2 19.0 %updates.1 = (f32[120,512]{1,0:T(8,128)}, f32[896,896]{1,0:T(8,128)}) custom-call(s32[1]{0:T(128)} %bitcast.first, s32[8]{0:T(128)} %pad_add_fusion.place_at, s32[4]{0:T(128)} %iota_xor_fusion.quarter_at, f32[1856,512]{1,0:T(8,128)} %all-gather.2.cloned.1.call-done.pieces_ref, f32[120,512]{1,0:T(8,128)} %bitcast.20, f32[512,512]{1,0:T(8,128)} %pivots.1.inverse_ref, ...), custom_call_target="tpu_custom_call" | custom-call | flops 2147483648 | bytes 12582912 | tf_op jit(solution)/shard_map/updates/pallas_call | solution.py:262
  293.2 6.6 %place.1 = f32[896,896]{1,0:T(8,128)} custom-call(f32[64,136,128]{2,1,0:T(8,128)} %all-to-all-done.incoming_hbm, f32[896,896]{1,0:T(8,128)} %get-tuple-element.5.base_ref), custom_call_target="tpu_custom_call" | custom-call | flops 2147483648 | bytes 12582912 | tf_op jit(solution)/shard_map/place/pallas_call | solution.py:316
  299.8 44.1 %reduce-scatter.2.cloned.1.call-done = f32[224,896]{1,0:T(8,128)} async-done(((f32[896,896]{1,0:T(8,128)}), f32[224,896]{1,0:T(8,128)}) %reduce-scatter.2.cloned.1.call-update) | async-done | bytes 802832 | tf_op jit(solution)/shard_map/reduce_scatter | solution.py:424
  (44 shorter events, 2.4 us)
Async XLA Ops:
  7.2 31.2 %collective-permute-start.5 = (f32[120,512]{1,0:T(8,128)}, f32[120,512]{1,0:T(8,128)S(1)}, u32[]{:S(2)}, u32[]{:S(2)}) collective-permute-start(f32[120,512]{1,0:T(8,128)} %bitcast.16), channel_id=1, source_target_pairs={{0,48},{1,49},{2,50},{3,51},{4,52},{5,53},{6,54},{7,55},{64,112},{... | collective-permute-start | bytes 737288 | tf_op jit(solution)/shard_map/ppermute | solution.py:372
  12.6 25.7 %collective-permute-start.4 = (f32[120,512]{1,0:T(8,128)}, f32[120,512]{1,0:T(8,128)S(1)}, u32[]{:S(2)}, u32[]{:S(2)}) collective-permute-start(f32[120,512]{1,0:T(8,128)} %bitcast.17), channel_id=1, source_target_pairs={{0,16},{1,17},{2,18},{3,19},{4,20},{5,21},{6,22},{7,23},{64,80},{6... | collective-permute-start | bytes 737288 | tf_op jit(solution)/shard_map/ppermute | solution.py:372
  14.0 24.4 %collective-permute-start.3 = (f32[120,512]{1,0:T(8,128)}, f32[120,512]{1,0:T(8,128)S(1)}, u32[]{:S(2)}, u32[]{:S(2)}) collective-permute-start(f32[120,512]{1,0:T(8,128)} %bitcast.18), channel_id=1, source_target_pairs={{0,8},{1,9},{2,10},{3,11},{4,12},{5,13},{6,14},{7,15},{64,72},{65,... | collective-permute-start | bytes 737288 | tf_op jit(solution)/shard_map/ppermute | solution.py:372
  18.2 18.8 %collective-permute-start = (f32[120,512]{1,0:T(8,128)}, f32[120,512]{1,0:T(8,128)S(1)}, u32[]{:S(2)}, u32[]{:S(2)}) collective-permute-start(f32[120,512]{1,0:T(8,128)} %bitcast.19), channel_id=1, source_target_pairs={{4,0},{5,1},{6,2},{7,3},{8,4},{9,6},{10,7},{11,8},{12,9},{13,10},{... | collective-permute-start | bytes 737288 | tf_op jit(solution)/shard_map/ppermute | solution.py:369
  20.2 18.1 %collective-permute-start.1 = (f32[8,512]{1,0:T(8,128)S(1)}, f32[8,512]{1,0:T(8,128)S(1)}, u32[]{:S(2)}, u32[]{:S(2)}) collective-permute-start(f32[8,512]{1,0:T(8,128)S(1)} %slice_bitcast_fusion), channel_id=1, source_target_pairs={{8,5},{22,20},{36,35},{50,50},{72,69},{86,84},{100,99},{114,114},{... | collective-permute-start | bytes 49160 | tf_op jit(solution)/shard_map/ppermute | solution.py:371
  20.9 9.8 %copy-start.8 = (s32[1,2,3]{2,1,0:T(2,128)S(1)}, s32[1,2,3]{2,1,0:T(2,128)}, u32[]{:S(2)}) copy-start(s32[1,2,3]{2,1,0:T(2,128)} %param.10) | copy-start | bytes 76
  20.9 16.1 %copy-start.4 = (f32[1,120,512]{2,1,0:T(8,128)S(1)}, f32[1,120,512]{2,1,0:T(8,128)}, u32[]{:S(2)}) copy-start(f32[1,120,512]{2,1,0:T(8,128)} %param.14) | copy-start | bytes 737284
  37.0 11.6 %collective-permute-start.2 = (f32[120,512]{1,0:T(8,128)S(1)}, f32[120,512]{1,0:T(8,128)S(1)}, u32[]{:S(2)}, u32[]{:S(2)}) collective-permute-start(f32[120,512]{1,0:T(8,128)S(1)} %bitcast.21), channel_id=1, source_target_pairs={{5,0},{6,1},{7,2},{9,5},{10,6},{11,7},{12,8},{13,9},{14,10},{15,11... | collective-permute-start | bytes 737288 | tf_op jit(solution)/shard_map/ppermute | solution.py:370
  61.5 6.0 %copy-start.1 = (f32[120,512]{1,0:T(8,128)S(1)}, f32[120,512]{1,0:T(8,128)}, u32[]{:S(2)}) copy-start(f32[120,512]{1,0:T(8,128)} %add_add_fusion.block_hbm) | copy-start | bytes 737284
  61.5 106.3 %copy-start.2 = (f32[112,512]{1,0:T(8,128)S(1)}, f32[112,512]{1,0:T(8,128)}, u32[]{:S(2)}) copy-start(f32[112,512]{1,0:T(8,128)} %get-tuple-element.9.chunk_hbm) | copy-start | bytes 688132
  61.5 231.7 %all-to-all-start = ((f32[64,136,128]{2,1,0:T(8,128)}), f32[64,136,128]{2,1,0:T(8,128)}, u32[]{:S(2)}, u32[]{:S(2)}) async-start(f32[64,136,128]{2,1,0:T(8,128)} %middles.1), calls=%async_computation | async-start | bytes 8912896 | tf_op jit(solution)/shard_map/all_to_all | solution.py:407
  67.4 180.2 %all-gather.2.cloned.1.call-start = ((), (), s32[]{:S(2)}) async-start(), calls=%async_computation.2 | async-start | bytes 5701632 | tf_op jit(solution)/shard_map/all_gather | solution.py:408
  67.5 100.2 %collective-permute-start.6 = (f32[120,512]{1,0:T(8,128)S(1)}, f32[120,512]{1,0:T(8,128)S(1)}, u32[]{:S(2)}, u32[]{:S(2)}) collective-permute-start(f32[120,512]{1,0:T(8,128)S(1)} %copy-done.1), channel_id=1, source_target_pairs={{8,24},{9,25},{10,26},{11,27},{12,28},{13,29},{14,30},{15,31},{16,... | collective-permute-start | bytes 737288 | tf_op jit(solution)/shard_map/ppermute | solution.py:384
  167.8 26.5 %collective-permute-start.7 = (f32[232,512]{1,0:T(8,128)S(1)}, f32[232,512]{1,0:T(8,128)S(1)}, u32[]{:S(2)}, u32[]{:S(2)}) collective-permute-start(f32[232,512]{1,0:T(8,128)S(1)} %pad_maximum_fusion), channel_id=1, source_target_pairs={{0,2},{1,3},{2,0},{3,1},{4,6},{5,7},{6,4},{7,5},{8,10},{9,11},{10,... | collective-permute-start | bytes 1425416 | tf_op jit(solution)/shard_map/ppermute | solution.py:402
  174.7 19.7 %collective-permute-start.8 = (f32[232,512]{1,0:T(8,128)S(1)}, f32[232,512]{1,0:T(8,128)S(1)}, u32[]{:S(2)}, u32[]{:S(2)}) collective-permute-start(f32[232,512]{1,0:T(8,128)S(1)} %pad_maximum_fusion), channel_id=1, source_target_pairs={{0,4},{1,5},{2,6},{3,7},{4,0},{5,1},{6,2},{7,3},{8,12},{9,13},{10,... | collective-permute-start | bytes 1425416 | tf_op jit(solution)/shard_map/ppermute | solution.py:402
  176.0 32.0 %collective-permute-start.9 = (f32[232,512]{1,0:T(8,128)S(1)}, f32[232,512]{1,0:T(8,128)S(1)}, u32[]{:S(2)}, u32[]{:S(2)}) collective-permute-start(f32[232,512]{1,0:T(8,128)S(1)} %pad_maximum_fusion), channel_id=1, source_target_pairs={{0,6},{1,7},{2,4},{3,5},{4,2},{5,3},{6,0},{7,1},{8,14},{9,15},{10,... | collective-permute-start | bytes 1425416 | tf_op jit(solution)/shard_map/ppermute | solution.py:402
  208.0 1.2 copy-start
  209.2 134.7 %reduce-scatter.2.cloned.1.call-start = ((), (), s32[]{:S(2)}) async-start(), calls=%async_computation.3 | async-start | bytes 4014080 | tf_op jit(solution)/shard_map/reduce_scatter | solution.py:424
  209.3 13.5 %collective-permute-start.10 = (f32[112,512]{1,0:T(8,128)S(1)}, f32[112,512]{1,0:T(8,128)S(1)}, u32[]{:S(2)}, u32[]{:S(2)}) collective-permute-start(f32[112,512]{1,0:T(8,128)S(1)} %copy-done.2), channel_id=1, source_target_pairs={{0,0},{1,8},{2,16},{3,24},{4,32},{5,40},{6,48},{7,56},{8,1},{9,9},... | collective-permute-start | bytes 688136 | tf_op jit(solution)/shard_map/ppermute | solution.py:378
  211.2 11.6 %collective-permute-start.11 = (f32[112,512]{1,0:T(8,128)S(1)}, f32[112,512]{1,0:T(8,128)S(1)}, u32[]{:S(2)}, u32[]{:S(2)}) collective-permute-start(f32[112,512]{1,0:T(8,128)S(1)} %copy-done.2), channel_id=1, source_target_pairs={{0,8},{1,0},{2,24},{3,16},{4,40},{5,32},{6,56},{7,48},{8,9},{9,1},... | collective-permute-start | bytes 688136 | tf_op jit(solution)/shard_map/ppermute | solution.py:381
  222.9 50.3 %copy-start.3 = (f32[224,512]{1,0:T(8,128)}, f32[224,512]{1,0:T(8,128)S(1)}, u32[]{:S(2)}) copy-start(f32[224,512]{1,0:T(8,128)S(1)} %maximum_select_fusion.rest_0_) | copy-start | bytes 1376260
  222.9 50.3 %collective-permute-start.14 = (f32[224,512]{1,0:T(8,128)S(1)}, f32[224,512]{1,0:T(8,128)S(1)}, u32[]{:S(2)}, u32[]{:S(2)}) collective-permute-start(f32[224,512]{1,0:T(8,128)S(1)} %maximum_select_fusion.rest_0_), channel_id=1, source_target_pairs={{0,48},{1,49},{2,50},{3,51},{4,52},{5,53},{6,54},{7,55},{8,56},{9,... | collective-permute-start | bytes 1376264 | tf_op jit(solution)/shard_map/ppermute | solution.py:405
  239.9 33.2 %collective-permute-start.13 = (f32[224,512]{1,0:T(8,128)S(1)}, f32[224,512]{1,0:T(8,128)S(1)}, u32[]{:S(2)}, u32[]{:S(2)}) collective-permute-start(f32[224,512]{1,0:T(8,128)S(1)} %maximum_select_fusion.rest_0_), channel_id=1, source_target_pairs={{0,32},{1,33},{2,34},{3,35},{4,36},{5,37},{6,38},{7,39},{8,40},{9,... | collective-permute-start | bytes 1376264 | tf_op jit(solution)/shard_map/ppermute | solution.py:405
  247.0 26.2 %collective-permute-start.12 = (f32[224,512]{1,0:T(8,128)S(1)}, f32[224,512]{1,0:T(8,128)S(1)}, u32[]{:S(2)}, u32[]{:S(2)}) collective-permute-start(f32[224,512]{1,0:T(8,128)S(1)} %maximum_select_fusion.rest_0_), channel_id=1, source_target_pairs={{0,16},{1,17},{2,18},{3,19},{4,20},{5,21},{6,22},{7,23},{8,24},{9,... | collective-permute-start | bytes 1376264 | tf_op jit(solution)/shard_map/ppermute | solution.py:405
  273.1 0.8 copy-start.5
  273.2 1.0 copy-start.6
  273.2 1.0 copy-start.7
Sparse Core Ops, SparseCore 0:
  209.3 36.3 all-gather.1
  299.9 43.9 reduce-scatter.1
where the time goes:
time: 351 us
  waiting for transfers between devices  190 us (54%)
  Pallas kernels  72.2 us (21%)
  starting transfers between devices  67.1 us (19%)
  between operations  15 us (4%)
  local copies, waits for them, and re-layouts  3.7 us (1%)
    ppermute x1, waiting for transfers between devices, program(): last = lax.ppermute(block, WIDE, across([(1, 3), (2, 4), (6, 7), (0, 5)]))  90.5 us
    reduce_scatter x1, waiting for transfers between devices, program(): top_part = lax.psum_scatter(total, 'grp', scatter_dimension=0, tiled=True)  44.1 us
    ppermute x3, waiting for transfers between devices, program(): lax.ppermute(mixed, WIDE, [(d, d ^ 2 * k) for d in range(64)])  30.8 us
    pallas_call x1, Pallas kernels, pivots(): pl.pallas_call(pivot_kernel, out_shape=jax.ShapeDtypeStruct((width, width...  25.5 us
    ppermute x3, starting transfers between devices, program(): lax.ppermute(pair, WIDE, [(d, d ^ 16 * k) for d in range(64)])  24.1 us
    pallas_call x1, Pallas kernels, updates(): pl.pallas_call(update_kernel, out_shape=(jax.ShapeDtypeStruct((PANEL, K *...  19 us
    pallas_call x1, Pallas kernels, middles(): pl.pallas_call(middle_kernel, out_shape=jax.ShapeDtypeStruct((64, SLOT, T...  12 us
    ppermute x3, starting transfers between devices, program(): spread = [lax.ppermute(panel, WIDE, across([(0, b)])) for b in (1, 2, 6)]  11 us
  transfers between devices with their start and end apart: 18, of which 7 were waited for; matrix products, arithmetic and copies ran while one was open for 1% of the time, Pallas kernels for 15%

commit v1 on v0

--- a/solution.py
+++ b/solution.py
@@ -14,7 +14,6 @@
 SLOT = 136
 PANEL = 120
 CHUNK = 112
-MIXED = PANEL + CHUNK
 SIDE = 896
 HI = lax.Precision.HIGHEST
 F32 = jnp.float32
@@ -82,7 +81,7 @@
 
 
 def middle_kernel(
-    leaf_live, leaf_map, mid_live, mid_map, leaf_ref, mid_hbm, chunk_hbm, block_hbm, out_hbm,
+    leaf_live, leaf_map, mid_live, mid_map, leaf_ref, mid_hbm, out_hbm,
     mid, update, spots, load_sem, send_sem, spot_sem,
 ):
     head = pltpu.make_async_copy(mid_hbm.at[:TILE], mid.at[:TILE], load_sem.at[0])
@@ -140,14 +139,14 @@
     mark.wait()
 
 
-def middles(leaf_live, leaf_map, mid_live, mid_map, leaf, mid, chunk, block):
+def middles(leaf_live, leaf_map, mid_live, mid_map, leaf, mid):
     smem = pl.BlockSpec(memory_space=pltpu.SMEM)
     vmem = pl.BlockSpec(memory_space=pltpu.VMEM)
     hbm = pl.BlockSpec(memory_space=pl.ANY)
     return pl.pallas_call(
         middle_kernel,
         out_shape=jax.ShapeDtypeStruct((64, SLOT, TILE), F32),
-        in_specs=[smem, smem, smem, smem, vmem, hbm, hbm, hbm],
+        in_specs=[smem, smem, smem, smem, vmem, hbm],
         out_specs=hbm,
         scratch_shapes=[
             pltpu.VMEM((1024, 1024), F32),
@@ -159,7 +158,7 @@
         ],
         cost_estimate=pl.CostEstimate(flops=COST, bytes_accessed=9 << 20, transcendentals=0),
         name="middles",
-    )(leaf_live, leaf_map, mid_live, mid_map, leaf, mid, chunk, block)
+    )(leaf_live, leaf_map, mid_live, mid_map, leaf, mid)
 
 
 def pivot_kernel(place_at, pieces_ref, inverse_ref, work, panel):
@@ -171,7 +170,7 @@
     work[:, width:] = eye
     for piece in range(8):
         at = place_at[piece]
-        part = pieces_ref[piece * MIXED + CHUNK : (piece + 1) * MIXED, :]
+        part = pieces_ref[piece * PANEL : (piece + 1) * PANEL, :]
 
         @pl.when(at < K)
         def _():
@@ -225,74 +224,107 @@
 
 
 def update_kernel(
-    first, place_at, quarter_at, pieces_ref, own_ref, inverse_ref, entry_ref, *rest
+    first, place_at, quarter_at, inverse_ref, own_ref, pieces_hbm, entry_hbm, *rest
 ):
-    quarter_refs, (panel_ref, out_ref, raw, high, low) = rest[:4], rest[4:]
+    quarter_hbms, rest = rest[:4], rest[4:]
+    panel_ref, out_hbm, raw, total, high, low, load_sem, entry_sem, store_sem = rest
     width = K * TILE
+    loads = [[], []]
+    for piece, hbm in enumerate(quarter_hbms):
+        at = pl.multiple_of(quarter_at[piece] * 2 * CHUNK, 8)
+        loads[1].append(
+            pltpu.make_async_copy(
+                hbm, raw.at[1, pl.ds(at, 2 * CHUNK), :], load_sem.at[1, piece]
+            )
+        )
+    for piece in range(8):
+        at = pl.multiple_of(place_at[piece] * CHUNK, 8)
+        loads[0].append(
+            pltpu.make_async_copy(
+                pieces_hbm.at[piece * CHUNK : (piece + 1) * CHUNK, :],
+                raw.at[0, pl.ds(at, CHUNK), :],
+                load_sem.at[0, piece],
+            )
+        )
+    entries = pltpu.make_async_copy(entry_hbm, total, entry_sem)
+    for copy in loads[1] + loads[0] + [entries]:
+        copy.start()
     inverse = inverse_ref[...]
     rows_at = first[0] + lax.broadcasted_iota(jnp.int32, (PANEL, width), 0)
     column = lax.broadcasted_iota(jnp.int32, (PANEL, width), 1)
     live = (column <= rows_at) | (rows_at >= width)
     panel_ref[...] = jnp.where(live, dot(own_ref[...], inverse, ((1,), (1,))), 0.0)
-    for piece in range(8):
-        raw[0, pl.ds(pl.multiple_of(place_at[piece] * CHUNK, 8), CHUNK), :] = pieces_ref[
-            piece * MIXED : piece * MIXED + CHUNK, :
-        ]
-    for piece, ref in enumerate(quarter_refs):
-        at = pl.multiple_of(quarter_at[piece] * 2 * CHUNK, 8)
-        raw[1, pl.ds(at, 2 * CHUNK), :] = ref[...]
-    for side in range(2):
+    for side in (1, 0):
+        for copy in loads[side]:
+            copy.wait()
         high[side], low[side] = split(dot(raw[side], inverse, ((1,), (1,))))
+    entries.wait()
 
     def product(lhs, rhs):
         return lax.dot_general(
             lhs, rhs, (((1,), (1,)), ((), ())), preferred_element_type=F32
         )
 
+    stores = []
     for t in range(7):
         at = slice(t * TILE, (t + 1) * TILE)
-        out_ref[at, :] = entry_ref[at, :] - (
+        total[at, :] = total[at, :] - (
             product(high[0, at, :], high[1])
             + (product(high[0, at, :], low[1]) + product(low[0, at, :], high[1]))
         )
-
-
-def updates(first, place_at, quarter_at, pieces, own, inverse, entries, quarters):
+        copy = pltpu.make_async_copy(total.at[at, :], out_hbm.at[at, :], store_sem.at[t])
+        copy.start()
+        stores.append(copy)
+    for copy in stores:
+        copy.wait()
+
+
+def updates(first, place_at, quarter_at, inverse, own, pieces, entries, quarters):
+    smem = pl.BlockSpec(memory_space=pltpu.SMEM)
     vmem = pl.BlockSpec(memory_space=pltpu.VMEM)
+    hbm = pl.BlockSpec(memory_space=pl.ANY)
     return pl.pallas_call(
         update_kernel,
         out_shape=(
             jax.ShapeDtypeStruct((PANEL, K * TILE), F32),
             jax.ShapeDtypeStruct((SIDE, SIDE), F32),
         ),
-        in_specs=[pl.BlockSpec(memory_space=pltpu.SMEM)] * 3 + [vmem] * 8,
-        out_specs=(vmem, vmem),
+        in_specs=[smem] * 3 + [vmem] * 2 + [hbm] * 6,
+        out_specs=(vmem, hbm),
         scratch_shapes=[
             pltpu.VMEM((2, SIDE, K * TILE), F32),
+            pltpu.VMEM((SIDE, SIDE), F32),
             pltpu.VMEM((2, SIDE, K * TILE), jnp.bfloat16),
             pltpu.VMEM((2, SIDE, K * TILE), jnp.bfloat16),
+            pltpu.SemaphoreType.DMA((2, 8)),
+            pltpu.SemaphoreType.DMA,
+            pltpu.SemaphoreType.DMA((7,)),
         ],
         cost_estimate=pl.CostEstimate(flops=COST, bytes_accessed=12 << 20, transcendentals=0),
         name="updates",
-    )(first, place_at, quarter_at, pieces, own, inverse, entries, *quarters)
-
-
-def place_kernel(incoming_hbm, base_ref, out_ref, incoming, spots, sem, spot_sem):
+    )(first, place_at, quarter_at, inverse, own, pieces, entries, *quarters)
+
+
+def place_kernel(
+    incoming_hbm, base_hbm, out_hbm, incoming, total, spots, sem, base_sem, store_sem, spot_sem
+):
     parts = 4
     count = 64 // parts
     mark = pltpu.make_async_copy(incoming_hbm.at[:, TILE, :], spots, spot_sem)
     mark.start()
+    base = pltpu.make_async_copy(base_hbm, total, base_sem)
+    base.start()
     copies = []
-    for part in range(parts):
-        at = pl.ds(part * count, count)
+    for piece in range(parts):
+        at = pl.ds(piece * count, count)
         copy = pltpu.make_async_copy(
-            incoming_hbm.at[at, :TILE, :], incoming.at[at], sem.at[part]
+            incoming_hbm.at[at, :TILE, :], incoming.at[at], sem.at[piece]
         )
         copy.start()
         copies.append(copy)
-    out_ref[...] = base_ref[...]
     mark.wait()
-    for part, copy in enumerate(copies):
+    base.wait()
+    for piece, copy in enumerate(copies):
         copy.wait()
 
         def body(s, carry):
@@ -302,29 +334,35 @@
             def _():
                 row = pl.multiple_of(((spot - 1) // 7) * TILE, TILE)
                 col = pl.multiple_of(((spot - 1) % 7) * TILE, TILE)
-                out_ref[pl.ds(row, TILE), pl.ds(col, TILE)] = (
-                    out_ref[pl.ds(row, TILE), pl.ds(col, TILE)] + incoming[s]
+                total[pl.ds(row, TILE), pl.ds(col, TILE)] = (
+                    total[pl.ds(row, TILE), pl.ds(col, TILE)] + incoming[s]
                 )
 
             return carry
 
-        lax.fori_loop(part * count, (part + 1) * count, body, 0)
+        lax.fori_loop(piece * count, (piece + 1) * count, body, 0)
+    store = pltpu.make_async_copy(total, out_hbm, store_sem)
+    store.start()
+    store.wait()
 
 
 def place(incoming, base):
-    vmem = pl.BlockSpec(memory_space=pltpu.VMEM)
+    hbm = pl.BlockSpec(memory_space=pl.ANY)
     return pl.pallas_call(
         place_kernel,
         out_shape=jax.ShapeDtypeStruct((SIDE, SIDE), F32),
-        in_specs=[pl.BlockSpec(memory_space=pl.ANY), vmem],
-        out_specs=vmem,
+        in_specs=[hbm, hbm],
+        out_specs=hbm,
         scratch_shapes=[
             pltpu.VMEM((64, TILE, TILE), F32),
+            pltpu.VMEM((SIDE, SIDE), F32),
             pltpu.SMEM((64, TILE), F32),
             pltpu.SemaphoreType.DMA((4,)),
             pltpu.SemaphoreType.DMA,
+            pltpu.SemaphoreType.DMA,
+            pltpu.SemaphoreType.DMA,
         ],
-        cost_estimate=pl.CostEstimate(flops=COST, bytes_accessed=12 << 20, transcendentals=0),
+        cost_estimate=pl.CostEstimate(flops=COST // 4, bytes_accessed=10 << 20, transcendentals=0),
         name="place",
     )(incoming, base)
 
@@ -389,8 +427,6 @@
         mid_map[0, 0],
         leaf_updates,
         mid_entries[0, 0],
-        chunk,
-        block,
     )
     pair = jnp.where(
         row % 2 == 0,
@@ -405,18 +441,21 @@
         lax.ppermute(pair, WIDE, [(d, d ^ (16 * k)) for d in range(64)]) for k in (1, 2, 3)
     ]
     incoming = lax.all_to_all(outgoing, WIDE, 0, 0, tiled=True)
-    pieces = lax.all_gather(jnp.concatenate(parts, axis=0), "c", axis=0, tiled=True)
+    pivot_parts = jnp.concatenate([part[CHUNK:] for part in parts], axis=0)
+    chunk_parts = jnp.concatenate([part[:CHUNK] for part in parts], axis=0)
+    pivot_pieces = lax.all_gather(pivot_parts, "c", axis=0, tiled=True)
+    pieces = lax.all_gather(chunk_parts, "c", axis=0, tiled=True)
     order = jnp.arange(4, dtype=jnp.int32)
     line = lax.axis_index("l") ^ order
     place_at = jnp.concatenate([2 * line, 2 * line + 1])
-    inverse = pivots(place_at, pieces)
+    inverse = pivots(place_at, pivot_pieces)
     root_panel, base = updates(
         (position * PANEL).reshape(1),
         place_at,
         lax.axis_index("y") ^ order,
+        inverse,
+        panel,
         pieces,
-        panel,
-        inverse,
         root_update_entries[0, 0],
         quarters,
     )

time: 351 us -> 341 us (0.972)
  starting transfers between devices: 67.1 us -> 42.6 us
  waiting for transfers between devices: 190 us -> 207 us
    ppermute x1, waiting for transfers between devices: 90.5 us -> 0.01 us  [program(): last = lax.ppermute(block, WIDE, across([(1, 3), (2, 4), (6, 7), (0, 5)]))]
    ppermute x3, waiting for transfers between devices: 0.01 us -> 88.5 us  [program(): spread = [lax.ppermute(panel, WIDE, across([(0, b)])) for b in (1, 2, 6)]]
    ppermute x1, waiting for transfers between devices: 5.8 us -> 30.7 us  [program(): head = lax.ppermute(panel, WIDE, first)]
    ppermute x3, starting transfers between devices: 24.1 us -> 8.31 us  [program(): lax.ppermute(pair, WIDE, [(d, d ^ 16 * k) for d in range(64)])]
    ppermute x1, waiting for transfers between devices: 9.45 us -> 0.01 us  [program(): tail = lax.ppermute(panel, WIDE, second)]
    ppermute x1, starting transfers between devices: 9.74 us -> 1.3 us  [program(): last = lax.ppermute(block, WIDE, across([(1, 3), (2, 4), (6, 7), (0, 5)]))]
    all_to_all x1, starting transfers between devices: 5.94 us -> 13.3 us  [program(): incoming = lax.all_to_all(outgoing, WIDE, 0, 0, tiled=True)]
    ppermute x3, starting transfers between devices: 9.24 us -> 3.63 us  [program(): lax.ppermute(mixed, WIDE, [(d, d ^ 2 * k) for d in range(64)])]
  transfers between devices with their start and end apart: 18 -> 19, of which waited for: 7 -> 8; matrix products, arithmetic and copies ran while one was open for 1% -> 1% of each run, Pallas kernels for 15% -> 12%
where the time goes in v1:
time: 341 us
  waiting for transfers between devices  207 us (61%)
  Pallas kernels  69.7 us (20%)
  starting transfers between devices  42.6 us (12%)
  between operations  14.8 us (4%)
  other arithmetic  3.57 us (1%)
    ppermute x3, waiting for transfers between devices, program(): spread = [lax.ppermute(panel, WIDE, across([(0, b)])) for b in (1, 2, 6)]  88.5 us
    reduce_scatter x1, waiting for transfers between devices, program(): top_part = lax.psum_scatter(total, 'grp', scatter_dimension=0, tiled=True)  43.5 us
    ppermute x3, waiting for transfers between devices, program(): lax.ppermute(mixed, WIDE, [(d, d ^ 2 * k) for d in range(64)])  34 us
    ppermute x1, waiting for transfers between devices, program(): head = lax.ppermute(panel, WIDE, first)  30.7 us
    pallas_call x1, Pallas kernels, pivots(): pl.pallas_call(pivot_kernel, out_shape=jax.ShapeDtypeStruct((width, width...  25 us
    pallas_call x1, Pallas kernels, updates(): pl.pallas_call(update_kernel, out_shape=(jax.ShapeDtypeStruct((PANEL, K *...  17.4 us
    all_to_all x1, starting transfers between devices, program(): incoming = lax.all_to_all(outgoing, WIDE, 0, 0, tiled=True)  13.3 us
    pallas_call x1, Pallas kernels, middles(): pl.pallas_call(middle_kernel, out_shape=jax.ShapeDtypeStruct((64, SLOT, T...  12 us
  transfers between devices with their start and end apart: 19, of which 8 were waited for; matrix products, arithmetic and copies ran while one was open for 1% of the time, Pallas kernels for 12%

profile of v1, /device:TPU:1, one launch (start us, length us, event | category | flops | bytes accessed | tf_op | source)
XLA Modules:
  0.0 340.5 jit_solution(10812062933453392164)
XLA Ops:
  7.8 1.3 reshape_squeeze.3.leaf_map
  9.1 9.0 %leaves.1.leaf_ref = f32[2,384,384]{2,1,0:T(8,128)} custom-call(f32[2,512,512]{2,1,0:T(8,128)} %bitcast.24), custom_call_target="tpu_custom_call" | custom-call | flops 2147483648 | bytes 3145728 | tf_op jit(solution)/shard_map/leaves/pallas_call | solution.py:74
  18.1 12.0 %middles.1 = f32[64,136,128]{2,1,0:T(8,128)} custom-call(s32[2]{0:T(128)} %bitcast.22, s32[6]{0:T(128)} %reshape_squeeze.3.leaf_map, s32[1]{0:T(128)} %bitcast.13.mid_live, s32[7]{0:T(128)} %bitcast.23, f32[2,384,384]{2,1,0:T(8,128)} %leaves.1.leaf_ref, f32[1024,1024]{1,0:T(8,128)} %bitcast.14), custom_call_target="tpu_custom_call" | custom-call | flops 2147483648 | bytes 9437184 | tf_op jit(solution)/shard_map/middles/pallas_call | solution.py:146
  30.2 13.3 %all-to-all-start = ((f32[64,136,128]{2,1,0:T(8,128)}), f32[64,136,128]{2,1,0:T(8,128)}, u32[]{:S(2)}, u32[]{:S(2)}) async-start(f32[64,136,128]{2,1,0:T(8,128)} %middles.1), calls=%async_computation | async-start | bytes 8912896 | tf_op jit(solution)/shard_map/all_to_all | solution.py:443
  43.5 4.7 %collective-permute-start.2 = (f32[120,512]{1,0:T(8,128)S(1)}, f32[120,512]{1,0:T(8,128)S(1)}, u32[]{:S(2)}, u32[]{:S(2)}) collective-permute-start(f32[120,512]{1,0:T(8,128)S(1)} %bitcast.17), channel_id=1, source_target_pairs={{0,48},{1,49},{2,50},{3,51},{4,52},{5,53},{6,54},{7,55},{64,112},{... | collective-permute-start | bytes 737288 | tf_op jit(solution)/shard_map/ppermute | solution.py:410
  48.2 1.3 collective-permute-start.1
  49.5 2.5 collective-permute-start
  52.1 1.3 collective-permute-start.6
  53.4 1.3 collective-permute-start.4
  54.7 7.8 %collective-permute-done.2 = f32[120,512]{1,0:T(8,128)S(1)} collective-permute-done((f32[120,512]{1,0:T(8,128)S(1)}, f32[120,512]{1,0:T(8,128)S(1)}, u32[]{:S(2)}, u32[]{:S(2)}) %collective-permute-start.2) | collective-permute-done | bytes 245792 | tf_op jit(solution)/shard_map/ppermute | solution.py:410
  62.5 0.7 collective-permute-start.5
  63.2 80.7 %collective-permute-done = f32[120,512]{1,0:T(8,128)S(1)} collective-permute-done((f32[120,512]{1,0:T(8,128)S(1)}, f32[120,512]{1,0:T(8,128)S(1)}, u32[]{:S(2)}, u32[]{:S(2)}) %collective-permute-start) | collective-permute-done | bytes 245792 | tf_op jit(solution)/shard_map/ppermute | solution.py:410
  144.0 1.3 collective-permute-start.3
  145.3 30.7 %collective-permute-done.4 = f32[120,512]{1,0:T(8,128)S(1)} collective-permute-done((f32[120,512]{1,0:T(8,128)S(1)}, f32[120,512]{1,0:T(8,128)S(1)}, u32[]{:S(2)}, u32[]{:S(2)}) %collective-permute-start.4) | collective-permute-done | bytes 245792 | tf_op jit(solution)/shard_map/ppermute | solution.py:407
  176.4 2.0 collective-permute-start.8
  178.4 1.5 collective-permute-start.7
  179.9 9.1 %collective-permute-done.9 = f32[232,512]{1,0:T(8,128)S(1)} collective-permute-done((f32[232,512]{1,0:T(8,128)S(1)}, f32[232,512]{1,0:T(8,128)S(1)}, u32[]{:S(2)}, u32[]{:S(2)}) %collective-permute-start.9) | collective-permute-done | bytes 475168 | tf_op jit(solution)/shard_map/ppermute | solution.py:438
  189.1 24.9 %collective-permute-done.8 = f32[232,512]{1,0:T(8,128)S(1)} collective-permute-done((f32[232,512]{1,0:T(8,128)S(1)}, f32[232,512]{1,0:T(8,128)S(1)}, u32[]{:S(2)}, u32[]{:S(2)}) %collective-permute-start.8) | collective-permute-done | bytes 475168 | tf_op jit(solution)/shard_map/ppermute | solution.py:438
  214.0 1.0 pad_maximum_fusion
  215.2 1.0 pad_maximum_fusion.1
  216.3 4.1 %collective-permute-start.10 = (f32[112,512]{1,0:T(8,128)S(1)}, f32[112,512]{1,0:T(8,128)S(1)}, u32[]{:S(2)}, u32[]{:S(2)}) collective-permute-start(f32[112,512]{1,0:T(8,128)S(1)} %fusion.1), channel_id=1, source_target_pairs={{0,0},{1,8},{2,16},{3,24},{4,32},{5,40},{6,48},{7,56},{8,1},{9,9},... | collective-permute-start | bytes 688136 | tf_op jit(solution)/shard_map/ppermute | solution.py:416
  220.5 0.6 iota_xor_fusion.quarter_at
  221.1 9.4 %collective-permute-done.10 = f32[112,512]{1,0:T(8,128)S(1)} collective-permute-done((f32[112,512]{1,0:T(8,128)S(1)}, f32[112,512]{1,0:T(8,128)S(1)}, u32[]{:S(2)}, u32[]{:S(2)}) %collective-permute-start.10) | collective-permute-done | bytes 229408 | tf_op jit(solution)/shard_map/ppermute | solution.py:416
  230.4 1.3 collective-permute-done.11
  231.8 7.6 %collective-permute-start.14 = (f32[224,512]{1,0:T(8,128)S(1)}, f32[224,512]{1,0:T(8,128)S(1)}, u32[]{:S(2)}, u32[]{:S(2)}) collective-permute-start(f32[224,512]{1,0:T(8,128)S(1)} %maximum_select_fusion.rest_0_), channel_id=1, source_target_pairs={{0,48},{1,49},{2,50},{3,51},{4,52},{5,53},{6,54},{7,55},{8,56},{9,... | collective-permute-start | bytes 1376264 | tf_op jit(solution)/shard_map/ppermute | solution.py:441
  239.5 0.7 collective-permute-start.12
  240.1 0.6 pad_add_fusion.place_at
  240.8 25.0 %pivots.1.inverse_ref = f32[512,512]{1,0:T(8,128)} custom-call(s32[8]{0:T(128)} %pad_add_fusion.place_at, f32[960,512]{1,0:T(8,128)} %all-gather.3.cloned.1.call-done.pieces_ref), custom_call_target="tpu_custom_call" | custom-call | flops 4294967296 | bytes 2097152 | tf_op jit(solution)/shard_map/pivots/pallas_call | solution.py:207
  265.9 0.7 copy-done.2
  266.9 17.4 %updates.1 = (f32[120,512]{1,0:T(8,128)}, f32[896,896]{1,0:T(8,128)}) custom-call(s32[1]{0:T(128)} %bitcast.first, s32[8]{0:T(128)} %pad_add_fusion.place_at, s32[4]{0:T(128)} %iota_xor_fusion.quarter_at, f32[512,512]{1,0:T(8,128)} %pivots.1.inverse_ref, f32[120,512]{1,0:T(8,128)} %bitcast.16, f32[896,512]{1,0:T(8,128)} %all-gather.5.cloned.1.call-done.pieces_hbm, ...), custom_call_target="tpu_custom_call" | custom-call | flops 2147483648 | bytes 12582912 | tf_op jit(solution)/shard_map/updates/pallas_call | solution.py:286
  284.3 6.2 %place.1 = f32[896,896]{1,0:T(8,128)} custom-call(f32[64,136,128]{2,1,0:T(8,128)} %all-to-all-done.incoming_hbm, f32[896,896]{1,0:T(8,128)} %get-tuple-element.5.base_hbm), custom_call_target="tpu_custom_call" | custom-call | flops 536870912 | bytes 10485760 | tf_op jit(solution)/shard_map/place/pallas_call | solution.py:351
  290.6 43.5 %reduce-scatter.2.cloned.1.call-done = f32[224,896]{1,0:T(8,128)} async-done(((f32[896,896]{1,0:T(8,128)}), f32[224,896]{1,0:T(8,128)}) %reduce-scatter.2.cloned.1.call-update) | async-done | bytes 802832 | tf_op jit(solution)/shard_map/reduce_scatter | solution.py:463
  (44 shorter events, 1.2 us)
Async XLA Ops:
  30.2 13.3 %copy-start.1 = (f32[1,120,512]{2,1,0:T(8,128)S(1)}, f32[1,120,512]{2,1,0:T(8,128)}, u32[]{:S(2)}) copy-start(f32[1,120,512]{2,1,0:T(8,128)} %param.14) | copy-start | bytes 737284
  30.2 254.1 %all-to-all-start = ((f32[64,136,128]{2,1,0:T(8,128)}), f32[64,136,128]{2,1,0:T(8,128)}, u32[]{:S(2)}, u32[]{:S(2)}) async-start(f32[64,136,128]{2,1,0:T(8,128)} %middles.1), calls=%async_computation | async-start | bytes 8912896 | tf_op jit(solution)/shard_map/all_to_all | solution.py:443
  43.4 197.3 %all-gather.3.cloned.1.call-start = ((), (), s32[]{:S(2)}) async-start(), calls=%async_computation.2 | async-start | bytes 2949120 | tf_op jit(solution)/shard_map/all_gather | solution.py:446
  43.5 19.0 %collective-permute-start.2 = (f32[120,512]{1,0:T(8,128)S(1)}, f32[120,512]{1,0:T(8,128)S(1)}, u32[]{:S(2)}, u32[]{:S(2)}) collective-permute-start(f32[120,512]{1,0:T(8,128)S(1)} %bitcast.17), channel_id=1, source_target_pairs={{0,48},{1,49},{2,50},{3,51},{4,52},{5,53},{6,54},{7,55},{64,112},{... | collective-permute-start | bytes 737288 | tf_op jit(solution)/shard_map/ppermute | solution.py:410
  48.2 15.0 %collective-permute-start.1 = (f32[120,512]{1,0:T(8,128)S(1)}, f32[120,512]{1,0:T(8,128)S(1)}, u32[]{:S(2)}, u32[]{:S(2)}) collective-permute-start(f32[120,512]{1,0:T(8,128)S(1)} %bitcast.18), channel_id=1, source_target_pairs={{0,16},{1,17},{2,18},{3,19},{4,20},{5,21},{6,22},{7,23},{64,80},{6... | collective-permute-start | bytes 737288 | tf_op jit(solution)/shard_map/ppermute | solution.py:410
  49.5 94.4 %collective-permute-start = (f32[120,512]{1,0:T(8,128)S(1)}, f32[120,512]{1,0:T(8,128)S(1)}, u32[]{:S(2)}, u32[]{:S(2)}) collective-permute-start(f32[120,512]{1,0:T(8,128)S(1)} %bitcast.19), channel_id=1, source_target_pairs={{0,8},{1,9},{2,10},{3,11},{4,12},{5,13},{6,14},{7,15},{64,72},{65,... | collective-permute-start | bytes 737288 | tf_op jit(solution)/shard_map/ppermute | solution.py:410
  52.1 124.0 %collective-permute-start.6 = (f32[120,512]{1,0:T(8,128)S(1)}, f32[120,512]{1,0:T(8,128)S(1)}, u32[]{:S(2)}, u32[]{:S(2)}) collective-permute-start(f32[120,512]{1,0:T(8,128)S(1)} %bitcast.20), channel_id=1, source_target_pairs={{5,0},{6,1},{7,2},{9,5},{10,6},{11,7},{12,8},{13,9},{14,10},{15,11... | collective-permute-start | bytes 737288 | tf_op jit(solution)/shard_map/ppermute | solution.py:408
  53.4 122.7 %collective-permute-start.4 = (f32[120,512]{1,0:T(8,128)S(1)}, f32[120,512]{1,0:T(8,128)S(1)}, u32[]{:S(2)}, u32[]{:S(2)}) collective-permute-start(f32[120,512]{1,0:T(8,128)S(1)} %bitcast.21), channel_id=1, source_target_pairs={{4,0},{5,1},{6,2},{7,3},{8,4},{9,6},{10,7},{11,8},{12,9},{13,10},{... | collective-permute-start | bytes 737288 | tf_op jit(solution)/shard_map/ppermute | solution.py:407
  62.5 113.5 %collective-permute-start.5 = (f32[8,512]{1,0:T(8,128)S(1)}, f32[8,512]{1,0:T(8,128)S(1)}, u32[]{:S(2)}, u32[]{:S(2)}) collective-permute-start(f32[8,512]{1,0:T(8,128)S(1)} %slice_bitcast_fusion), channel_id=1, source_target_pairs={{8,5},{22,20},{36,35},{50,50},{72,69},{86,84},{100,99},{114,114},{... | collective-permute-start | bytes 49160 | tf_op jit(solution)/shard_map/ppermute | solution.py:409
  144.0 32.2 %collective-permute-start.3 = (f32[120,512]{1,0:T(8,128)S(1)}, f32[120,512]{1,0:T(8,128)S(1)}, u32[]{:S(2)}, u32[]{:S(2)}) collective-permute-start(f32[120,512]{1,0:T(8,128)S(1)} %add_add_fusion), channel_id=1, source_target_pairs={{8,24},{9,25},{10,26},{11,27},{12,28},{13,29},{14,30},{15,31},{16,... | collective-permute-start | bytes 737288 | tf_op jit(solution)/shard_map/ppermute | solution.py:422
  176.3 12.7 %collective-permute-start.9 = (f32[232,512]{1,0:T(8,128)S(1)}, f32[232,512]{1,0:T(8,128)S(1)}, u32[]{:S(2)}, u32[]{:S(2)}) collective-permute-start(f32[232,512]{1,0:T(8,128)S(1)} %pad_maximum_fusion.2), channel_id=1, source_target_pairs={{0,6},{1,7},{2,4},{3,5},{4,2},{5,3},{6,0},{7,1},{8,14},{9,15},{10,... | collective-permute-start | bytes 1425416 | tf_op jit(solution)/shard_map/ppermute | solution.py:438
  176.4 37.6 %collective-permute-start.8 = (f32[232,512]{1,0:T(8,128)S(1)}, f32[232,512]{1,0:T(8,128)S(1)}, u32[]{:S(2)}, u32[]{:S(2)}) collective-permute-start(f32[232,512]{1,0:T(8,128)S(1)} %pad_maximum_fusion.2), channel_id=1, source_target_pairs={{0,4},{1,5},{2,6},{3,7},{4,0},{5,1},{6,2},{7,3},{8,12},{9,13},{10,... | collective-permute-start | bytes 1425416 | tf_op jit(solution)/shard_map/ppermute | solution.py:438
  178.4 35.6 %collective-permute-start.7 = (f32[232,512]{1,0:T(8,128)S(1)}, f32[232,512]{1,0:T(8,128)S(1)}, u32[]{:S(2)}, u32[]{:S(2)}) collective-permute-start(f32[232,512]{1,0:T(8,128)S(1)} %pad_maximum_fusion.2), channel_id=1, source_target_pairs={{0,2},{1,3},{2,0},{3,1},{4,6},{5,7},{6,4},{7,5},{8,10},{9,11},{10,... | collective-permute-start | bytes 1425416 | tf_op jit(solution)/shard_map/ppermute | solution.py:438
  215.1 50.8 %all-gather.5.cloned.1.call-start = ((), (), s32[]{:S(2)}) async-start(), calls=%async_computation.3 | async-start | bytes 2752512 | tf_op jit(solution)/shard_map/all_gather | solution.py:447
  216.2 117.8 %reduce-scatter.2.cloned.1.call-start = ((), (), s32[]{:S(2)}) async-start(), calls=%async_computation.4 | async-start | bytes 4014080 | tf_op jit(solution)/shard_map/reduce_scatter | solution.py:463
  216.3 14.2 %collective-permute-start.10 = (f32[112,512]{1,0:T(8,128)S(1)}, f32[112,512]{1,0:T(8,128)S(1)}, u32[]{:S(2)}, u32[]{:S(2)}) collective-permute-start(f32[112,512]{1,0:T(8,128)S(1)} %fusion.1), channel_id=1, source_target_pairs={{0,0},{1,8},{2,16},{3,24},{4,32},{5,40},{6,48},{7,56},{8,1},{9,9},... | collective-permute-start | bytes 688136 | tf_op jit(solution)/shard_map/ppermute | solution.py:416
  220.4 11.4 %collective-permute-start.11 = (f32[112,512]{1,0:T(8,128)S(1)}, f32[112,512]{1,0:T(8,128)S(1)}, u32[]{:S(2)}, u32[]{:S(2)}) collective-permute-start(f32[112,512]{1,0:T(8,128)S(1)} %fusion.1), channel_id=1, source_target_pairs={{0,8},{1,0},{2,24},{3,16},{4,40},{5,32},{6,56},{7,48},{8,9},{9,1},... | collective-permute-start | bytes 688136 | tf_op jit(solution)/shard_map/ppermute | solution.py:419
  231.8 34.0 %copy-start = (f32[224,512]{1,0:T(8,128)}, f32[224,512]{1,0:T(8,128)S(1)}, u32[]{:S(2)}) copy-start(f32[224,512]{1,0:T(8,128)S(1)} %maximum_select_fusion.rest_0_) | copy-start | bytes 1376260
  231.8 34.0 %collective-permute-start.14 = (f32[224,512]{1,0:T(8,128)S(1)}, f32[224,512]{1,0:T(8,128)S(1)}, u32[]{:S(2)}, u32[]{:S(2)}) collective-permute-start(f32[224,512]{1,0:T(8,128)S(1)} %maximum_select_fusion.rest_0_), channel_id=1, source_target_pairs={{0,48},{1,49},{2,50},{3,51},{4,52},{5,53},{6,54},{7,55},{8,56},{9,... | collective-permute-start | bytes 1376264 | tf_op jit(solution)/shard_map/ppermute | solution.py:441
  239.5 26.4 %collective-permute-start.13 = (f32[224,512]{1,0:T(8,128)S(1)}, f32[224,512]{1,0:T(8,128)S(1)}, u32[]{:S(2)}, u32[]{:S(2)}) collective-permute-start(f32[224,512]{1,0:T(8,128)S(1)} %maximum_select_fusion.rest_0_), channel_id=1, source_target_pairs={{0,32},{1,33},{2,34},{3,35},{4,36},{5,37},{6,38},{7,39},{8,40},{9,... | collective-permute-start | bytes 1376264 | tf_op jit(solution)/shard_map/ppermute | solution.py:441
  239.5 26.4 %collective-permute-start.12 = (f32[224,512]{1,0:T(8,128)S(1)}, f32[224,512]{1,0:T(8,128)S(1)}, u32[]{:S(2)}, u32[]{:S(2)}) collective-permute-start(f32[224,512]{1,0:T(8,128)S(1)} %maximum_select_fusion.rest_0_), channel_id=1, source_target_pairs={{0,16},{1,17},{2,18},{3,19},{4,20},{5,21},{6,22},{7,23},{8,24},{9,... | collective-permute-start | bytes 1376264 | tf_op jit(solution)/shard_map/ppermute | solution.py:441
  265.8 0.8 copy-start.2
  265.8 0.9 copy-start.3
  265.8 1.1 copy-start.4
Sparse Core Ops, SparseCore 0:
  215.2 22.0 all-gather.2
  239.1 16.8 all-gather.4
  290.7 43.2 reduce-scatter.1

commit v2 on v1

--- a/solution.py
+++ b/solution.py
@@ -12,6 +12,7 @@
 K = 4
 BLK = 16
 SLOT = 136
+HOLDERS = 5
 PANEL = 120
 CHUNK = 112
 SIDE = 896
@@ -90,21 +91,27 @@
     rest.start()
 
     def assemble(in_head):
-        for i in range(2):
-            live = leaf_live[i]
-            for a in range(UL):
-                to_row = leaf_map[i * UL + a]
-                row = pl.multiple_of(to_row * TILE, TILE)
-                wanted = (to_row == 0) if in_head else (to_row > 0)
-                for b in range(UL):
-                    col = pl.multiple_of(leaf_map[i * UL + b] * TILE, TILE)
-
-                    @pl.when(wanted & (a < live) & (b < live))
-                    def _():
-                        mid[pl.ds(row, TILE), pl.ds(col, TILE)] = (
-                            mid[pl.ds(row, TILE), pl.ds(col, TILE)]
-                            + leaf_ref[i, a * TILE : (a + 1) * TILE, b * TILE : (b + 1) * TILE]
-                        )
+        def body(n, carry):
+            i = n // (UL * UL)
+            a = (n // UL) % UL
+            b = n % UL
+            to_row = leaf_map[i * UL + a]
+            row = pl.multiple_of(to_row * TILE, TILE)
+            col = pl.multiple_of(leaf_map[i * UL + b] * TILE, TILE)
+            from_row = pl.multiple_of(a * TILE, TILE)
+            from_col = pl.multiple_of(b * TILE, TILE)
+            wanted = (to_row == 0) if in_head else (to_row > 0)
+
+            @pl.when(wanted & (a < leaf_live[i]) & (b < leaf_live[i]))
+            def _():
+                mid[pl.ds(row, TILE), pl.ds(col, TILE)] = (
+                    mid[pl.ds(row, TILE), pl.ds(col, TILE)]
+                    + leaf_ref[i, pl.ds(from_row, TILE), pl.ds(from_col, TILE)]
+                )
+
+            return carry
+
+        lax.fori_loop(0, 2 * UL * UL, body, 0)
 
     head.wait()
     assemble(True)
@@ -224,39 +231,24 @@
 
 
 def update_kernel(
-    first, place_at, quarter_at, inverse_ref, own_ref, pieces_hbm, entry_hbm, *rest
+    first, inverse_ref, own_ref, rows_hbm, cols_hbm, entry_hbm, panel_ref, out_hbm,
+    raw, total, high, low, load_sem, entry_sem, store_sem,
 ):
-    quarter_hbms, rest = rest[:4], rest[4:]
-    panel_ref, out_hbm, raw, total, high, low, load_sem, entry_sem, store_sem = rest
     width = K * TILE
-    loads = [[], []]
-    for piece, hbm in enumerate(quarter_hbms):
-        at = pl.multiple_of(quarter_at[piece] * 2 * CHUNK, 8)
-        loads[1].append(
-            pltpu.make_async_copy(
-                hbm, raw.at[1, pl.ds(at, 2 * CHUNK), :], load_sem.at[1, piece]
-            )
-        )
-    for piece in range(8):
-        at = pl.multiple_of(place_at[piece] * CHUNK, 8)
-        loads[0].append(
-            pltpu.make_async_copy(
-                pieces_hbm.at[piece * CHUNK : (piece + 1) * CHUNK, :],
-                raw.at[0, pl.ds(at, CHUNK), :],
-                load_sem.at[0, piece],
-            )
-        )
+    loads = [
+        pltpu.make_async_copy(hbm, raw.at[side], load_sem.at[side])
+        for side, hbm in enumerate((rows_hbm, cols_hbm))
+    ]
     entries = pltpu.make_async_copy(entry_hbm, total, entry_sem)
-    for copy in loads[1] + loads[0] + [entries]:
+    for copy in loads + [entries]:
         copy.start()
     inverse = inverse_ref[...]
     rows_at = first[0] + lax.broadcasted_iota(jnp.int32, (PANEL, width), 0)
     column = lax.broadcasted_iota(jnp.int32, (PANEL, width), 1)
     live = (column <= rows_at) | (rows_at >= width)
     panel_ref[...] = jnp.where(live, dot(own_ref[...], inverse, ((1,), (1,))), 0.0)
-    for side in (1, 0):
-        for copy in loads[side]:
-            copy.wait()
+    for side in range(2):
+        loads[side].wait()
         high[side], low[side] = split(dot(raw[side], inverse, ((1,), (1,))))
     entries.wait()
 
@@ -279,7 +271,7 @@
         copy.wait()
 
 
-def updates(first, place_at, quarter_at, inverse, own, pieces, entries, quarters):
+def updates(first, inverse, own, rows, cols, entries):
     smem = pl.BlockSpec(memory_space=pltpu.SMEM)
     vmem = pl.BlockSpec(memory_space=pltpu.VMEM)
     hbm = pl.BlockSpec(memory_space=pl.ANY)
@@ -289,20 +281,20 @@
             jax.ShapeDtypeStruct((PANEL, K * TILE), F32),
             jax.ShapeDtypeStruct((SIDE, SIDE), F32),
         ),
-        in_specs=[smem] * 3 + [vmem] * 2 + [hbm] * 6,
+        in_specs=[smem] + [vmem] * 2 + [hbm] * 3,
         out_specs=(vmem, hbm),
         scratch_shapes=[
             pltpu.VMEM((2, SIDE, K * TILE), F32),
             pltpu.VMEM((SIDE, SIDE), F32),
             pltpu.VMEM((2, SIDE, K * TILE), jnp.bfloat16),
             pltpu.VMEM((2, SIDE, K * TILE), jnp.bfloat16),
-            pltpu.SemaphoreType.DMA((2, 8)),
+            pltpu.SemaphoreType.DMA((2,)),
             pltpu.SemaphoreType.DMA,
             pltpu.SemaphoreType.DMA((7,)),
         ],
         cost_estimate=pl.CostEstimate(flops=COST, bytes_accessed=12 << 20, transcendentals=0),
         name="updates",
-    )(first, place_at, quarter_at, inverse, own, pieces, entries, *quarters)
+    )(first, inverse, own, rows, cols, entries)
 
 
 def place_kernel(
@@ -387,7 +379,7 @@
 
 
 def across(pairs):
-    return [(a * 8 + q, b * 8 + q) for a, b in pairs for q in range(8)]
+    return [(a * 8 + q, b * 8 + q) for a, b in pairs for q in range(HOLDERS)]
 
 
 def program(
@@ -433,31 +425,28 @@
         jnp.concatenate([straight, crossed], axis=0),
         jnp.concatenate([crossed, straight], axis=0),
     )
-    mixed = jnp.concatenate([chunk, block + last], axis=0)
-    parts = [mixed] + [
-        lax.ppermute(mixed, WIDE, [(d, d ^ (2 * k)) for d in range(64)]) for k in (1, 2, 3)
-    ]
-    quarters = [pair] + [
-        lax.ppermute(pair, WIDE, [(d, d ^ (16 * k)) for d in range(64)]) for k in (1, 2, 3)
+    block = block + last
+    parts = [block] + [
+        lax.ppermute(
+            block, WIDE, [(d, d ^ (2 * k)) for d in range(64) if d % 8 < HOLDERS]
+        )
+        for k in (1, 2, 3)
     ]
     incoming = lax.all_to_all(outgoing, WIDE, 0, 0, tiled=True)
-    pivot_parts = jnp.concatenate([part[CHUNK:] for part in parts], axis=0)
-    chunk_parts = jnp.concatenate([part[:CHUNK] for part in parts], axis=0)
-    pivot_pieces = lax.all_gather(pivot_parts, "c", axis=0, tiled=True)
-    pieces = lax.all_gather(chunk_parts, "c", axis=0, tiled=True)
+    rows = lax.all_gather(chunk, ("l", "c"), axis=0, tiled=True)
+    pivot_pieces = lax.all_gather(jnp.concatenate(parts, axis=0), "c", axis=0, tiled=True)
+    cols = lax.all_gather(pair, "y", axis=0, tiled=True)
     order = jnp.arange(4, dtype=jnp.int32)
     line = lax.axis_index("l") ^ order
     place_at = jnp.concatenate([2 * line, 2 * line + 1])
     inverse = pivots(place_at, pivot_pieces)
     root_panel, base = updates(
         (position * PANEL).reshape(1),
-        place_at,
-        lax.axis_index("y") ^ order,
         inverse,
         panel,
-        pieces,
+        rows,
+        cols,
         root_update_entries[0, 0],
-        quarters,
     )
     total = place(incoming, base)
     top_part = lax.psum_scatter(total, "grp", scatter_dimension=0, tiled=True)

time: 341 us -> 358 us (1.050)
  waiting for transfers between devices: 207 us -> 224 us
    ppermute x1, waiting for transfers between devices: 0.01 us -> 90.3 us  [program(): last = lax.ppermute(block, WIDE, across([(1, 3), (2, 4), (6, 7), (0, 5)]))]
    ppermute x3, waiting for transfers between devices: 88.5 us -> 0.01 us  [program(): spread = [lax.ppermute(panel, WIDE, across([(0, b)])) for b in (1, 2, 6)]]
    all_gather x2 -> x3, waiting for transfers between devices: 0.02 us -> 51.8 us  [the longest x1 38.4 us: program(): rows = lax.all_gather(chunk, ('l', 'c'), axis=0, tiled=True)]
    ppermute x6 -> x3, waiting for transfers between devices: 34 us -> 6.39 us  [program(): lax.ppermute(block, WIDE, [(d, d ^ 2 * k) for d in range(64) if d % 8 < H...]
    ppermute x1, waiting for transfers between devices: 30.7 us -> 5.18 us  [program(): head = lax.ppermute(panel, WIDE, first)]
    ppermute x1, waiting for transfers between devices: 0.01 us -> 17.6 us  [program(): tail = lax.ppermute(panel, WIDE, second)]
    ppermute x1, starting transfers between devices: 1.3 us -> 9.85 us  [program(): last = lax.ppermute(block, WIDE, across([(1, 3), (2, 4), (6, 7), (0, 5)]))]
    all_to_all x1, starting transfers between devices: 13.3 us -> 5.67 us  [program(): incoming = lax.all_to_all(outgoing, WIDE, 0, 0, tiled=True)]
  transfers between devices with their start and end apart: 19 -> 17, of which waited for: 8 -> 10; matrix products, arithmetic and copies ran while one was open for 1% -> 1% of each run, Pallas kernels for 12% -> 18%
where the time goes in v2:
time: 358 us
  waiting for transfers between devices  224 us (63%)
  Pallas kernels  70.5 us (20%)
  starting transfers between devices  45.5 us (13%)
  between operations  14.7 us (4%)
    ppermute x1, waiting for transfers between devices, program(): last = lax.ppermute(block, WIDE, across([(1, 3), (2, 4), (6, 7), (0, 5)]))  90.3 us
    reduce_scatter x1, waiting for transfers between devices, program(): top_part = lax.psum_scatter(total, 'grp', scatter_dimension=0, tiled=True)  42.9 us
    all_gather x1, waiting for transfers between devices, program(): rows = lax.all_gather(chunk, ('l', 'c'), axis=0, tiled=True)  38.4 us
    pallas_call x1, Pallas kernels, pivots(): pl.pallas_call(pivot_kernel, out_shape=jax.ShapeDtypeStruct((width, width...  25 us
    ppermute x1, waiting for transfers between devices, program(): tail = lax.ppermute(panel, WIDE, second)  17.6 us
    pallas_call x1, Pallas kernels, updates(): pl.pallas_call(update_kernel, out_shape=(jax.ShapeDtypeStruct((PANEL, K *...  17.3 us
    all_gather x1, waiting for transfers between devices, program(): cols = lax.all_gather(pair, 'y', axis=0, tiled=True)  13.3 us
    pallas_call x1, Pallas kernels, middles(): pl.pallas_call(middle_kernel, out_shape=jax.ShapeDtypeStruct((64, SLOT, T...  12.9 us
  transfers between devices with their start and end apart: 17, of which 10 were waited for; matrix products, arithmetic and copies ran while one was open for 1% of the time, Pallas kernels for 18%

profile of v2, /device:TPU:1, one launch (start us, length us, event | category | flops | bytes accessed | tf_op | source)
XLA Modules:
  0.0 357.9 jit_solution(9540363835111298972)
XLA Ops:
  7.2 5.5 %collective-permute-start.2 = (f32[120,512]{1,0:T(8,128)}, f32[120,512]{1,0:T(8,128)S(1)}, u32[]{:S(2)}, u32[]{:S(2)}) collective-permute-start(f32[120,512]{1,0:T(8,128)} %bitcast.16), channel_id=1, source_target_pairs={{0,48},{1,49},{2,50},{3,51},{4,52},{64,112},{65,113},{66,114},{67,... | collective-permute-start | bytes 737288 | tf_op jit(solution)/shard_map/ppermute | solution.py:402
  12.6 1.3 collective-permute-start.1
  14.0 4.2 %collective-permute-start = (f32[120,512]{1,0:T(8,128)}, f32[120,512]{1,0:T(8,128)S(1)}, u32[]{:S(2)}, u32[]{:S(2)}) collective-permute-start(f32[120,512]{1,0:T(8,128)} %bitcast.18), channel_id=1, source_target_pairs={{0,8},{1,9},{2,10},{3,11},{4,12},{64,72},{65,73},{66,74},{67,75},{... | collective-permute-start | bytes 737288 | tf_op jit(solution)/shard_map/ppermute | solution.py:402
  18.2 9.1 %leaves.1.leaf_ref = f32[2,384,384]{2,1,0:T(8,128)} custom-call(f32[2,512,512]{2,1,0:T(8,128)} %bitcast.24), custom_call_target="tpu_custom_call" | custom-call | flops 2147483648 | bytes 3145728 | tf_op jit(solution)/shard_map/leaves/pallas_call | solution.py:75
  27.9 0.6 reshape_squeeze.3.leaf_map
  28.5 12.9 %middles.1 = f32[64,136,128]{2,1,0:T(8,128)} custom-call(s32[2]{0:T(128)} %bitcast.22, s32[6]{0:T(128)} %reshape_squeeze.3.leaf_map, s32[1]{0:T(128)} %bitcast.13.mid_live, s32[7]{0:T(128)} %bitcast.23, f32[2,384,384]{2,1,0:T(8,128)} %leaves.1.leaf_ref, f32[1024,1024]{1,0:T(8,128)} %bitcast.14), custom_call_target="tpu_custom_call" | custom-call | flops 2147483648 | bytes 9437184 | tf_op jit(solution)/shard_map/middles/pallas_call | solution.py:153
  41.4 5.7 %all-to-all-start = ((f32[64,136,128]{2,1,0:T(8,128)}), f32[64,136,128]{2,1,0:T(8,128)}, u32[]{:S(2)}, u32[]{:S(2)}) async-start(f32[64,136,128]{2,1,0:T(8,128)} %middles.1), calls=%async_computation | async-start | bytes 8912896 | tf_op jit(solution)/shard_map/all_to_all | solution.py:435
  47.3 9.9 %collective-permute-start.3 = (f32[120,512]{1,0:T(8,128)S(1)}, f32[120,512]{1,0:T(8,128)S(1)}, u32[]{:S(2)}, u32[]{:S(2)}) collective-permute-start(f32[120,512]{1,0:T(8,128)S(1)} %add_add_fusion), channel_id=1, source_target_pairs={{8,24},{9,25},{10,26},{11,27},{12,28},{16,32},{17,33},{18,34},{19,... | collective-permute-start | bytes 737288 | tf_op jit(solution)/shard_map/ppermute | solution.py:414
  57.2 90.3 %collective-permute-done.3 = f32[120,512]{1,0:T(8,128)S(1)} collective-permute-done((f32[120,512]{1,0:T(8,128)S(1)}, f32[120,512]{1,0:T(8,128)S(1)}, u32[]{:S(2)}, u32[]{:S(2)}) %collective-permute-start.3) | collective-permute-done | bytes 245792 | tf_op jit(solution)/shard_map/ppermute | solution.py:414
  147.5 1.3 collective-permute-start.6
  148.8 1.3 collective-permute-start.5
  150.1 3.3 collective-permute-start.4
  153.5 3.8 %collective-permute-done.5 = f32[120,512]{1,0:T(8,128)S(1)} collective-permute-done((f32[120,512]{1,0:T(8,128)S(1)}, f32[120,512]{1,0:T(8,128)S(1)}, u32[]{:S(2)}, u32[]{:S(2)}) %collective-permute-start.5) | collective-permute-done | bytes 245792 | tf_op jit(solution)/shard_map/ppermute | solution.py:430
  157.2 2.6 collective-permute-done.4
  159.9 1.0 pad_maximum_fusion
  161.0 1.3 collective-permute-start.7
  162.3 1.3 collective-permute-start.9
  163.6 0.7 collective-permute-start.8
  164.3 5.2 %collective-permute-done.7 = f32[120,512]{1,0:T(8,128)S(1)} collective-permute-done((f32[120,512]{1,0:T(8,128)S(1)}, f32[120,512]{1,0:T(8,128)S(1)}, u32[]{:S(2)}, u32[]{:S(2)}) %collective-permute-start.7) | collective-permute-done | bytes 245792 | tf_op jit(solution)/shard_map/ppermute | solution.py:399
  169.5 17.6 %collective-permute-done.9 = f32[120,512]{1,0:T(8,128)S(1)} collective-permute-done((f32[120,512]{1,0:T(8,128)S(1)}, f32[120,512]{1,0:T(8,128)S(1)}, u32[]{:S(2)}, u32[]{:S(2)}) %collective-permute-start.9) | collective-permute-done | bytes 245792 | tf_op jit(solution)/shard_map/ppermute | solution.py:400
  187.2 9.5 %collective-permute-start.10 = (f32[112,512]{1,0:T(8,128)S(1)}, f32[112,512]{1,0:T(8,128)S(1)}, u32[]{:S(2)}, u32[]{:S(2)}) collective-permute-start(f32[112,512]{1,0:T(8,128)S(1)} %fusion.1), channel_id=1, source_target_pairs={{0,0},{1,8},{2,16},{3,24},{4,32},{5,40},{6,48},{7,56},{8,1},{9,9},... | collective-permute-start | bytes 688136 | tf_op jit(solution)/shard_map/ppermute | solution.py:408
  196.9 4.6 %collective-permute-done.10 = f32[112,512]{1,0:T(8,128)S(1)} collective-permute-done((f32[112,512]{1,0:T(8,128)S(1)}, f32[112,512]{1,0:T(8,128)S(1)}, u32[]{:S(2)}, u32[]{:S(2)}) %collective-permute-start.10) | collective-permute-done | bytes 229408 | tf_op jit(solution)/shard_map/ppermute | solution.py:408
  201.5 4.3 %collective-permute-done.11 = f32[112,512]{1,0:T(8,128)S(1)} collective-permute-done((f32[112,512]{1,0:T(8,128)S(1)}, f32[112,512]{1,0:T(8,128)S(1)}, u32[]{:S(2)}, u32[]{:S(2)}) %collective-permute-start.11) | collective-permute-done | bytes 229408 | tf_op jit(solution)/shard_map/ppermute | solution.py:411
  205.8 0.8 maximum_select_fusion
  206.7 0.7 all-gather.6.cloned.1.call-update
  207.4 0.6 pad_add_fusion.place_at
  208.1 25.0 %pivots.1.inverse_ref = f32[512,512]{1,0:T(8,128)} custom-call(s32[8]{0:T(128)} %pad_add_fusion.place_at, f32[960,512]{1,0:T(8,128)} %all-gather.4.cloned.1.call-done.pieces_ref), custom_call_target="tpu_custom_call" | custom-call | flops 4294967296 | bytes 2097152 | tf_op jit(solution)/shard_map/pivots/pallas_call | solution.py:214
  233.1 13.3 %all-gather.8.cloned.1.call-done.cols_hbm = f32[896,512]{1,0:T(8,128)} async-done(((f32[224,512]{1,0:T(8,128)}), f32[896,512]{1,0:T(8,128)}) %all-gather.8.cloned.1.call-update) | async-done | bytes 1835024 | tf_op jit(solution)/shard_map/all_gather | solution.py:438
  246.4 38.4 %all-gather.6.cloned.1.call-done.rows_hbm = f32[896,512]{1,0:T(8,128)} async-done(((f32[112,512]{1,0:T(8,128)}), f32[896,512]{1,0:T(8,128)}) %all-gather.6.cloned.1.call-update) | async-done | bytes 1835024 | tf_op jit(solution)/shard_map/all_gather | solution.py:436
  284.9 17.3 %updates.1 = (f32[120,512]{1,0:T(8,128)}, f32[896,896]{1,0:T(8,128)}) custom-call(s32[1]{0:T(128)} %bitcast.first, f32[512,512]{1,0:T(8,128)} %pivots.1.inverse_ref, f32[120,512]{1,0:T(8,128)} %bitcast.19, f32[896,512]{1,0:T(8,128)} %all-gather.6.cloned.1.call-done.rows_hbm, f32[896,512]{1,0:T(8,128)} %all-gather.8.cloned.1.call-done.cols_hbm, ...), custom_call_target="tpu_custom_call" | custom-call | flops 2147483648 | bytes 12582912 | tf_op jit(solution)/shard_map/updates/pallas_call | solution.py:278
  302.2 6.2 %place.1 = f32[896,896]{1,0:T(8,128)} custom-call(f32[64,136,128]{2,1,0:T(8,128)} %all-to-all-done.incoming_hbm, f32[896,896]{1,0:T(8,128)} %get-tuple-element.5.base_hbm), custom_call_target="tpu_custom_call" | custom-call | flops 536870912 | bytes 10485760 | tf_op jit(solution)/shard_map/place/pallas_call | solution.py:343
  308.4 42.9 %reduce-scatter.2.cloned.1.call-done = f32[224,896]{1,0:T(8,128)} async-done(((f32[896,896]{1,0:T(8,128)}), f32[224,896]{1,0:T(8,128)}) %reduce-scatter.2.cloned.1.call-update) | async-done | bytes 802832 | tf_op jit(solution)/shard_map/reduce_scatter | solution.py:452
  (28 shorter events, 0.6 us)
Async XLA Ops:
  7.2 40.0 %collective-permute-start.2 = (f32[120,512]{1,0:T(8,128)}, f32[120,512]{1,0:T(8,128)S(1)}, u32[]{:S(2)}, u32[]{:S(2)}) collective-permute-start(f32[120,512]{1,0:T(8,128)} %bitcast.16), channel_id=1, source_target_pairs={{0,48},{1,49},{2,50},{3,51},{4,52},{64,112},{65,113},{66,114},{67,... | collective-permute-start | bytes 737288 | tf_op jit(solution)/shard_map/ppermute | solution.py:402
  12.6 34.5 %collective-permute-start.1 = (f32[120,512]{1,0:T(8,128)}, f32[120,512]{1,0:T(8,128)S(1)}, u32[]{:S(2)}, u32[]{:S(2)}) collective-permute-start(f32[120,512]{1,0:T(8,128)} %bitcast.17), channel_id=1, source_target_pairs={{0,16},{1,17},{2,18},{3,19},{4,20},{64,80},{65,81},{66,82},{67,83}... | collective-permute-start | bytes 737288 | tf_op jit(solution)/shard_map/ppermute | solution.py:402
  14.0 33.2 %collective-permute-start = (f32[120,512]{1,0:T(8,128)}, f32[120,512]{1,0:T(8,128)S(1)}, u32[]{:S(2)}, u32[]{:S(2)}) collective-permute-start(f32[120,512]{1,0:T(8,128)} %bitcast.18), channel_id=1, source_target_pairs={{0,8},{1,9},{2,10},{3,11},{4,12},{64,72},{65,73},{66,74},{67,75},{... | collective-permute-start | bytes 737288 | tf_op jit(solution)/shard_map/ppermute | solution.py:402
  18.2 9.7 %copy-start.2 = (s32[1,2,3]{2,1,0:T(2,128)S(1)}, s32[1,2,3]{2,1,0:T(2,128)}, u32[]{:S(2)}) copy-start(s32[1,2,3]{2,1,0:T(2,128)} %param.10) | copy-start | bytes 76
  41.4 5.8 %copy-start = (f32[1,120,512]{2,1,0:T(8,128)S(1)}, f32[1,120,512]{2,1,0:T(8,128)}, u32[]{:S(2)}) copy-start(f32[1,120,512]{2,1,0:T(8,128)} %param.14) | copy-start | bytes 737284
  41.4 260.7 %all-to-all-start = ((f32[64,136,128]{2,1,0:T(8,128)}), f32[64,136,128]{2,1,0:T(8,128)}, u32[]{:S(2)}, u32[]{:S(2)}) async-start(f32[64,136,128]{2,1,0:T(8,128)} %middles.1), calls=%async_computation | async-start | bytes 8912896 | tf_op jit(solution)/shard_map/all_to_all | solution.py:435
  47.1 161.0 %all-gather.4.cloned.1.call-start = ((), (), s32[]{:S(2)}) async-start(), calls=%async_computation.2 | async-start | bytes 2949120 | tf_op jit(solution)/shard_map/all_gather | solution.py:437
  47.3 100.2 %collective-permute-start.3 = (f32[120,512]{1,0:T(8,128)S(1)}, f32[120,512]{1,0:T(8,128)S(1)}, u32[]{:S(2)}, u32[]{:S(2)}) collective-permute-start(f32[120,512]{1,0:T(8,128)S(1)} %add_add_fusion), channel_id=1, source_target_pairs={{8,24},{9,25},{10,26},{11,27},{12,28},{16,32},{17,33},{18,34},{19,... | collective-permute-start | bytes 737288 | tf_op jit(solution)/shard_map/ppermute | solution.py:414
  147.5 6.0 %collective-permute-start.6 = (f32[120,512]{1,0:T(8,128)S(1)}, f32[120,512]{1,0:T(8,128)S(1)}, u32[]{:S(2)}, u32[]{:S(2)}) collective-permute-start(f32[120,512]{1,0:T(8,128)S(1)} %add.47), channel_id=1, source_target_pairs={{0,6},{1,7},{2,4},{3,5},{4,2},{8,14},{9,15},{10,12},{11,13},{12,10... | collective-permute-start | bytes 737288 | tf_op jit(solution)/shard_map/ppermute | solution.py:430
  148.8 8.4 %collective-permute-start.5 = (f32[120,512]{1,0:T(8,128)S(1)}, f32[120,512]{1,0:T(8,128)S(1)}, u32[]{:S(2)}, u32[]{:S(2)}) collective-permute-start(f32[120,512]{1,0:T(8,128)S(1)} %add.47), channel_id=1, source_target_pairs={{0,4},{1,5},{2,6},{3,7},{4,0},{8,12},{9,13},{10,14},{11,15},{12,8}... | collective-permute-start | bytes 737288 | tf_op jit(solution)/shard_map/ppermute | solution.py:430
  150.1 9.7 %collective-permute-start.4 = (f32[120,512]{1,0:T(8,128)S(1)}, f32[120,512]{1,0:T(8,128)S(1)}, u32[]{:S(2)}, u32[]{:S(2)}) collective-permute-start(f32[120,512]{1,0:T(8,128)S(1)} %add.47), channel_id=1, source_target_pairs={{0,2},{1,3},{2,0},{3,1},{4,6},{8,10},{9,11},{10,8},{11,9},{12,14},... | collective-permute-start | bytes 737288 | tf_op jit(solution)/shard_map/ppermute | solution.py:430
  160.9 85.5 %all-gather.8.cloned.1.call-start = ((), (), s32[]{:S(2)}) async-start(), calls=%async_computation.4 | async-start | bytes 2293760 | tf_op jit(solution)/shard_map/all_gather | solution.py:438
  161.0 8.5 %collective-permute-start.7 = (f32[120,512]{1,0:T(8,128)S(1)}, f32[120,512]{1,0:T(8,128)S(1)}, u32[]{:S(2)}, u32[]{:S(2)}) collective-permute-start(f32[120,512]{1,0:T(8,128)S(1)} %bitcast.20), channel_id=1, source_target_pairs={{4,0},{5,1},{6,2},{7,3},{8,4},{9,6},{10,7},{11,8},{12,9},{13,10},{... | collective-permute-start | bytes 737288 | tf_op jit(solution)/shard_map/ppermute | solution.py:399
  162.3 24.8 %collective-permute-start.9 = (f32[120,512]{1,0:T(8,128)S(1)}, f32[120,512]{1,0:T(8,128)S(1)}, u32[]{:S(2)}, u32[]{:S(2)}) collective-permute-start(f32[120,512]{1,0:T(8,128)S(1)} %bitcast.21), channel_id=1, source_target_pairs={{5,0},{6,1},{7,2},{9,5},{10,6},{11,7},{12,8},{13,9},{14,10},{15,11... | collective-permute-start | bytes 737288 | tf_op jit(solution)/shard_map/ppermute | solution.py:400
  163.6 5.9 %collective-permute-start.8 = (f32[8,512]{1,0:T(8,128)S(1)}, f32[8,512]{1,0:T(8,128)S(1)}, u32[]{:S(2)}, u32[]{:S(2)}) collective-permute-start(f32[8,512]{1,0:T(8,128)S(1)} %slice_bitcast_fusion), channel_id=1, source_target_pairs={{8,5},{22,20},{36,35},{50,50},{72,69},{86,84},{100,99},{114,114},{... | collective-permute-start | bytes 49160 | tf_op jit(solution)/shard_map/ppermute | solution.py:401
  187.2 19.4 %copy-start.1 = (f32[112,512]{1,0:T(8,128)}, f32[112,512]{1,0:T(8,128)S(1)}, u32[]{:S(2)}) copy-start(f32[112,512]{1,0:T(8,128)S(1)} %fusion.1) | copy-start | bytes 688132
  187.2 14.2 %collective-permute-start.10 = (f32[112,512]{1,0:T(8,128)S(1)}, f32[112,512]{1,0:T(8,128)S(1)}, u32[]{:S(2)}, u32[]{:S(2)}) collective-permute-start(f32[112,512]{1,0:T(8,128)S(1)} %fusion.1), channel_id=1, source_target_pairs={{0,0},{1,8},{2,16},{3,24},{4,32},{5,40},{6,48},{7,56},{8,1},{9,9},... | collective-permute-start | bytes 688136 | tf_op jit(solution)/shard_map/ppermute | solution.py:408
  196.8 9.0 %collective-permute-start.11 = (f32[112,512]{1,0:T(8,128)S(1)}, f32[112,512]{1,0:T(8,128)S(1)}, u32[]{:S(2)}, u32[]{:S(2)}) collective-permute-start(f32[112,512]{1,0:T(8,128)S(1)} %fusion.1), channel_id=1, source_target_pairs={{0,8},{1,0},{2,24},{3,16},{4,40},{5,32},{6,56},{7,48},{8,9},{9,1},... | collective-permute-start | bytes 688136 | tf_op jit(solution)/shard_map/ppermute | solution.py:411
  206.6 78.2 %all-gather.6.cloned.1.call-start = ((), (), s32[]{:S(2)}) async-start(), calls=%async_computation.3 | async-start | bytes 2064384 | tf_op jit(solution)/shard_map/all_gather | solution.py:436
  207.4 144.0 %reduce-scatter.2.cloned.1.call-start = ((), (), s32[]{:S(2)}) async-start(), calls=%async_computation.5 | async-start | bytes 4014080 | tf_op jit(solution)/shard_map/reduce_scatter | solution.py:452
Sparse Core Ops, SparseCore 0:
  161.0 30.9 all-gather.3
  206.7 39.6 all-gather.7
  248.8 36.0 all-gather.5
  308.5 42.7 reduce-scatter.1

commit v3 on v2

--- a/solution.py
+++ b/solution.py
@@ -168,24 +168,14 @@
     )(leaf_live, leaf_map, mid_live, mid_map, leaf, mid)
 
 
-def pivot_kernel(place_at, pieces_ref, inverse_ref, work, panel):
+def pivot_kernel(pieces_ref, inverse_ref, work, panel):
     width = K * TILE
     eye = (
         lax.broadcasted_iota(jnp.int32, (width, width), 0)
         == lax.broadcasted_iota(jnp.int32, (width, width), 1)
     ).astype(F32)
     work[:, width:] = eye
-    for piece in range(8):
-        at = place_at[piece]
-        part = pieces_ref[piece * PANEL : (piece + 1) * PANEL, :]
-
-        @pl.when(at < K)
-        def _():
-            work[pl.ds(pl.multiple_of(at * PANEL, 8), PANEL), :width] = part
-
-        @pl.when(at == K)
-        def _():
-            work[K * PANEL : width, :width] = part[: width - K * PANEL]
+    work[:, :width] = pieces_ref[:width, :]
 
     def step(k, carry):
         base = pl.multiple_of(k * TILE, TILE)
@@ -208,13 +198,13 @@
     inverse_ref[...] = work[:, width:]
 
 
-def pivots(place_at, pieces):
+def pivots(pieces):
     width = K * TILE
     vmem = pl.BlockSpec(memory_space=pltpu.VMEM)
     return pl.pallas_call(
         pivot_kernel,
         out_shape=jax.ShapeDtypeStruct((width, width), F32),
-        in_specs=[pl.BlockSpec(memory_space=pltpu.SMEM), vmem],
+        in_specs=[vmem],
         out_specs=vmem,
         scratch_shapes=[
             pltpu.VMEM((width, 2 * width), F32),
@@ -222,7 +212,7 @@
         ],
         cost_estimate=pl.CostEstimate(flops=2 * COST, bytes_accessed=2 << 20, transcendentals=0),
         name="pivots",
-    )(place_at, pieces)
+    )(pieces)
 
 
 def split(value):
@@ -231,16 +221,21 @@
 
 
 def update_kernel(
-    first, inverse_ref, own_ref, rows_hbm, cols_hbm, entry_hbm, panel_ref, out_hbm,
-    raw, total, high, low, load_sem, entry_sem, store_sem,
+    first, quarter_at, inverse_ref, own_ref, rows_hbm, entry_hbm, *rest
 ):
+    quarter_hbms, rest = rest[:4], rest[4:]
+    panel_ref, out_hbm, raw, total, high, low, load_sem, entry_sem, store_sem = rest
     width = K * TILE
-    loads = [
-        pltpu.make_async_copy(hbm, raw.at[side], load_sem.at[side])
-        for side, hbm in enumerate((rows_hbm, cols_hbm))
-    ]
+    loads = [[pltpu.make_async_copy(rows_hbm, raw.at[0], load_sem.at[0])], []]
+    for piece, hbm in enumerate(quarter_hbms):
+        at = pl.multiple_of(quarter_at[piece] * 2 * CHUNK, 8)
+        loads[1].append(
+            pltpu.make_async_copy(
+                hbm, raw.at[1, pl.ds(at, 2 * CHUNK), :], load_sem.at[1 + piece]
+            )
+        )
     entries = pltpu.make_async_copy(entry_hbm, total, entry_sem)
-    for copy in loads + [entries]:
+    for copy in loads[0] + loads[1] + [entries]:
         copy.start()
     inverse = inverse_ref[...]
     rows_at = first[0] + lax.broadcasted_iota(jnp.int32, (PANEL, width), 0)
@@ -248,7 +243,8 @@
     live = (column <= rows_at) | (rows_at >= width)
     panel_ref[...] = jnp.where(live, dot(own_ref[...], inverse, ((1,), (1,))), 0.0)
     for side in range(2):
-        loads[side].wait()
+        for copy in loads[side]:
+            copy.wait()
         high[side], low[side] = split(dot(raw[side], inverse, ((1,), (1,))))
     entries.wait()
 
@@ -271,7 +267,7 @@
         copy.wait()
 
 
-def updates(first, inverse, own, rows, cols, entries):
+def updates(first, quarter_at, inverse, own, rows, entries, quarters):
     smem = pl.BlockSpec(memory_space=pltpu.SMEM)
     vmem = pl.BlockSpec(memory_space=pltpu.VMEM)
     hbm = pl.BlockSpec(memory_space=pl.ANY)
@@ -281,20 +277,20 @@
             jax.ShapeDtypeStruct((PANEL, K * TILE), F32),
             jax.ShapeDtypeStruct((SIDE, SIDE), F32),
         ),
-        in_specs=[smem] + [vmem] * 2 + [hbm] * 3,
+        in_specs=[smem] * 2 + [vmem] * 2 + [hbm] * 6,
         out_specs=(vmem, hbm),
         scratch_shapes=[
             pltpu.VMEM((2, SIDE, K * TILE), F32),
             pltpu.VMEM((SIDE, SIDE), F32),
             pltpu.VMEM((2, SIDE, K * TILE), jnp.bfloat16),
             pltpu.VMEM((2, SIDE, K * TILE), jnp.bfloat16),
-            pltpu.SemaphoreType.DMA((2,)),
+            pltpu.SemaphoreType.DMA((5,)),
             pltpu.SemaphoreType.DMA,
             pltpu.SemaphoreType.DMA((7,)),
         ],
         cost_estimate=pl.CostEstimate(flops=COST, bytes_accessed=12 << 20, transcendentals=0),
         name="updates",
-    )(first, inverse, own, rows, cols, entries)
+    )(first, quarter_at, inverse, own, rows, entries, *quarters)
 
 
 def place_kernel(
@@ -378,10 +374,6 @@
     return first, second, third
 
 
-def across(pairs):
-    return [(a * 8 + q, b * 8 + q) for a, b in pairs for q in range(HOLDERS)]
-
-
 def program(
     leaf_entries,
     leaf_tiles,
@@ -396,22 +388,25 @@
     row = position // 8
     panel = root_panel_entries[0]
     first, second, third = rechunk_pairs()
+    crossing = lax.ppermute(panel, WIDE, [(q, 8 + q) for q in range(HOLDERS)])
     head = lax.ppermute(panel, WIDE, first)
     tail = lax.ppermute(panel, WIDE, second)
     extra = lax.ppermute(panel[CHUNK:], WIDE, third)
-    spread = [lax.ppermute(panel, WIDE, across([(0, b)])) for b in (1, 2, 6)]
     leaf_updates = leaves(leaf_entries[0])
     joined = jnp.concatenate([head[:CHUNK], head[CHUNK:] + extra, tail], axis=0)
     offset = (K * TILE + CHUNK * position) % PANEL
     chunk = lax.dynamic_slice_in_dim(joined, offset, CHUNK, 0)
-    block = jnp.where(row == 0, panel, 0.0) + (spread[0] + spread[1] + spread[2])
+    block = jnp.where(row % 2 == 0, panel, crossing)
+    block = lax.all_gather(
+        jnp.concatenate([block, jnp.zeros((16, K * TILE), F32)], axis=0), "y", axis=0
+    )[0, :PANEL]
+    pivot_pieces = lax.all_gather(block, ("l", "c"), axis=0, tiled=True)
     straight = lax.ppermute(
         chunk, WIDE, [(p * 8 + q, q * 8 + p) for p in range(8) for q in range(8)]
     )
     crossed = lax.ppermute(
         chunk, WIDE, [(p * 8 + q, (q ^ 1) * 8 + p) for p in range(8) for q in range(8)]
     )
-    last = lax.ppermute(block, WIDE, across([(1, 3), (2, 4), (6, 7), (0, 5)]))
     outgoing = middles(
         leaf_tiles[0],
         leaf_map[0].reshape(-1),
@@ -425,28 +420,20 @@
         jnp.concatenate([straight, crossed], axis=0),
         jnp.concatenate([crossed, straight], axis=0),
     )
-    block = block + last
-    parts = [block] + [
-        lax.ppermute(
-            block, WIDE, [(d, d ^ (2 * k)) for d in range(64) if d % 8 < HOLDERS]
-        )
-        for k in (1, 2, 3)
+    quarters = [pair] + [
+        lax.ppermute(pair, WIDE, [(d, d ^ (16 * k)) for d in range(64)]) for k in (1, 2, 3)
     ]
     incoming = lax.all_to_all(outgoing, WIDE, 0, 0, tiled=True)
     rows = lax.all_gather(chunk, ("l", "c"), axis=0, tiled=True)
-    pivot_pieces = lax.all_gather(jnp.concatenate(parts, axis=0), "c", axis=0, tiled=True)
-    cols = lax.all_gather(pair, "y", axis=0, tiled=True)
-    order = jnp.arange(4, dtype=jnp.int32)
-    line = lax.axis_index("l") ^ order
-    place_at = jnp.concatenate([2 * line, 2 * line + 1])
-    inverse = pivots(place_at, pivot_pieces)
+    inverse = pivots(pivot_pieces)
     root_panel, base = updates(
         (position * PANEL).reshape(1),
+        lax.axis_index("y") ^ jnp.arange(4, dtype=jnp.int32),
         inverse,
         panel,
         rows,
-        cols,
         root_update_entries[0, 0],
+        quarters,
     )
     total = place(incoming, base)
     top_part = lax.psum_scatter(total, "grp", scatter_dimension=0, tiled=True)

time: 358 us -> 310 us (0.87)
  waiting for transfers between devices: 224 us -> 182 us
  starting transfers between devices: 45.5 us -> 37.1 us
    ppermute x7 -> x4, waiting for transfers between devices: 96.7 us -> 0.01 us  [the longest x3 0.01 us: program(): lax.ppermute(pair, WIDE, [(d, d ^ 16 * k) for d in range(64)])]
    ppermute x1, waiting for transfers between devices: 5.18 us -> 75.3 us  [program(): head = lax.ppermute(panel, WIDE, first)]
    all_gather x1, waiting for transfers between devices: 38.4 us -> 0.02 us  [program(): rows = lax.all_gather(chunk, ('l', 'c'), axis=0, tiled=True)]
    all_gather x2, waiting for transfers between devices: 13.3 us -> 34.8 us  [the longest x1 34.8 us: program(): lax.all_gather(jnp.concatenate([block, jnp.zeros((16, K * TILE), F32)], a...]
    ppermute x7 -> x4, starting transfers between devices: 26.8 us -> 20.4 us  [the longest x3 10.8 us: program(): lax.ppermute(pair, WIDE, [(d, d ^ 16 * k) for d in range(64)])]
    ppermute x1, waiting for transfers between devices: 4.58 us -> 9.25 us  [program(): lax.ppermute(chunk, WIDE, [(p * 8 + q, q * 8 + p) for p in range(8) for q...]
  transfers between devices with their start and end apart: 17 -> 14, of which waited for: 10 -> 6; matrix products, arithmetic and copies ran while one was open for 1% -> 1% of each run, Pallas kernels for 18% -> 21%
where the time goes in v3:
time: 310 us
  waiting for transfers between devices  182 us (59%)
  Pallas kernels  70.4 us (23%)
  starting transfers between devices  37.1 us (12%)
  between operations  14.7 us (5%)
  local copies, waits for them, and re-layouts  4.02 us (1%)
    ppermute x1, waiting for transfers between devices, program(): head = lax.ppermute(panel, WIDE, first)  75.3 us
    reduce_scatter x1, waiting for transfers between devices, program(): top_part = lax.psum_scatter(total, 'grp', scatter_dimension=0, tiled=True)  43.7 us
    all_gather x1, waiting for transfers between devices, program(): lax.all_gather(jnp.concatenate([block, jnp.zeros((16, K * TILE), F32)], a...  34.8 us
    pallas_call x1, Pallas kernels, pivots(): pl.pallas_call(pivot_kernel, out_shape=jax.ShapeDtypeStruct((width, width...  24.9 us
    ppermute x1, waiting for transfers between devices, program(): tail = lax.ppermute(panel, WIDE, second)  17.6 us
    pallas_call x1, Pallas kernels, updates(): pl.pallas_call(update_kernel, out_shape=(jax.ShapeDtypeStruct((PANEL, K *...  17.3 us
    pallas_call x1, Pallas kernels, middles(): pl.pallas_call(middle_kernel, out_shape=jax.ShapeDtypeStruct((64, SLOT, T...  12.9 us
    ppermute x3, starting transfers between devices, program(): lax.ppermute(pair, WIDE, [(d, d ^ 16 * k) for d in range(64)])  10.8 us
  transfers between devices with their start and end apart: 14, of which 6 were waited for; matrix products, arithmetic and copies ran while one was open for 1% of the time, Pallas kernels for 21%

profile of v3, /device:TPU:1, one launch (start us, length us, event | category | flops | bytes accessed | tf_op | source)
XLA Modules:
  0.0 309.8 jit_solution(15266332123408753637)
XLA Ops:
  7.2 9.6 %collective-permute-start = (f32[120,512]{1,0:T(8,128)}, f32[120,512]{1,0:T(8,128)S(1)}, u32[]{:S(2)}, u32[]{:S(2)}) collective-permute-start(f32[120,512]{1,0:T(8,128)} %bitcast.18), channel_id=1, source_target_pairs={{0,8},{1,9},{2,10},{3,11},{4,12},{64,72},{65,73},{66,74},{67,75},{... | collective-permute-start | bytes 737288 | tf_op jit(solution)/shard_map/ppermute | solution.py:391
  16.8 9.1 %leaves.1.leaf_ref = f32[2,384,384]{2,1,0:T(8,128)} custom-call(f32[2,512,512]{2,1,0:T(8,128)} %bitcast.25), custom_call_target="tpu_custom_call" | custom-call | flops 2147483648 | bytes 3145728 | tf_op jit(solution)/shard_map/leaves/pallas_call | solution.py:75
  26.6 0.6 reshape_squeeze.3.leaf_map
  27.1 12.9 %middles.1 = f32[64,136,128]{2,1,0:T(8,128)} custom-call(s32[2]{0:T(128)} %bitcast.23, s32[6]{0:T(128)} %reshape_squeeze.3.leaf_map, s32[1]{0:T(128)} %bitcast.15.mid_live, s32[7]{0:T(128)} %bitcast.24, f32[2,384,384]{2,1,0:T(8,128)} %leaves.1.leaf_ref, f32[1024,1024]{1,0:T(8,128)} %bitcast.16), custom_call_target="tpu_custom_call" | custom-call | flops 2147483648 | bytes 9437184 | tf_op jit(solution)/shard_map/middles/pallas_call | solution.py:153
  40.1 5.7 %all-to-all-start = ((f32[64,136,128]{2,1,0:T(8,128)}), f32[64,136,128]{2,1,0:T(8,128)}, u32[]{:S(2)}, u32[]{:S(2)}) async-start(f32[64,136,128]{2,1,0:T(8,128)} %middles.1), calls=%async_computation | async-start | bytes 8912896 | tf_op jit(solution)/shard_map/all_to_all | solution.py:426
  45.8 0.0 all-gather.8.cloned.1.call-start
  45.9 0.7 concatenate.12
  46.7 0.0 all-gather.10.cloned.1.call-start
  46.7 34.8 %all-gather.8.cloned.1.call-done = f32[544,512]{1,0:T(8,128)} async-done(((f32[136,512]{1,0:T(8,128)}), f32[544,512]{1,0:T(8,128)}) %all-gather.8.cloned.1.call-update) | async-done | bytes 1114128 | tf_op jit(solution)/shard_map/all_gather | solution.py:400
  81.5 1.7 slice.20
  83.1 0.0 all-gather.6.cloned.1.call-start
  83.2 1.3 collective-permute-start.1
  84.5 1.3 collective-permute-start.3
  85.8 0.7 collective-permute-start.2
  86.5 75.3 %collective-permute-done.1 = f32[120,512]{1,0:T(8,128)S(1)} collective-permute-done((f32[120,512]{1,0:T(8,128)S(1)}, f32[120,512]{1,0:T(8,128)S(1)}, u32[]{:S(2)}, u32[]{:S(2)}) %collective-permute-start.1) | collective-permute-done | bytes 245792 | tf_op jit(solution)/shard_map/ppermute | solution.py:392
  161.8 17.6 %collective-permute-done.3 = f32[120,512]{1,0:T(8,128)S(1)} collective-permute-done((f32[120,512]{1,0:T(8,128)S(1)}, f32[120,512]{1,0:T(8,128)S(1)}, u32[]{:S(2)}, u32[]{:S(2)}) %collective-permute-start.3) | collective-permute-done | bytes 245792 | tf_op jit(solution)/shard_map/ppermute | solution.py:393
  179.5 0.8 fusion.1
  180.3 0.0 reduce-scatter.2.cloned.1.call-start
  180.3 7.5 %collective-permute-start.4 = (f32[112,512]{1,0:T(8,128)}, f32[112,512]{1,0:T(8,128)S(1)}, u32[]{:S(2)}, u32[]{:S(2)}) collective-permute-start(f32[112,512]{1,0:T(8,128)} %fusion.1), channel_id=1, source_target_pairs={{0,0},{1,8},{2,16},{3,24},{4,32},{5,40},{6,48},{7,56},{8,1},{9,9},... | collective-permute-start | bytes 688136 | tf_op jit(solution)/shard_map/ppermute | solution.py:404
  187.8 0.1 collective-permute-start.5
  187.9 9.3 %collective-permute-done.4 = f32[112,512]{1,0:T(8,128)S(1)} collective-permute-done((f32[112,512]{1,0:T(8,128)}, f32[112,512]{1,0:T(8,128)S(1)}, u32[]{:S(2)}, u32[]{:S(2)}) %collective-permute-start.4) | collective-permute-done | bytes 229408 | tf_op jit(solution)/shard_map/ppermute | solution.py:404
  197.2 1.5 collective-permute-done.5
  198.7 8.3 %collective-permute-start.8 = (f32[224,512]{1,0:T(8,128)S(1)}, f32[224,512]{1,0:T(8,128)S(1)}, u32[]{:S(2)}, u32[]{:S(2)}) collective-permute-start(f32[224,512]{1,0:T(8,128)S(1)} %maximum_select_fusion.rest_0_), channel_id=1, source_target_pairs={{0,48},{1,49},{2,50},{3,51},{4,52},{5,53},{6,54},{7,55},{8,56},{9,... | collective-permute-start | bytes 1376264 | tf_op jit(solution)/shard_map/ppermute | solution.py:424
  207.0 2.5 collective-permute-start.7
  209.4 0.5 iota_xor_fusion.quarter_at
  210.0 24.9 %pivots.1.inverse_ref = f32[512,512]{1,0:T(8,128)} custom-call(f32[960,512]{1,0:T(8,128)} %bitcast.26), custom_call_target="tpu_custom_call" | custom-call | flops 4294967296 | bytes 2097152 | tf_op jit(solution)/shard_map/pivots/pallas_call | solution.py:204
  235.0 0.7 copy-done.2
  235.7 0.1 copy-done.3
  235.8 0.2 copy-done.4
  236.0 17.3 %updates.1 = (f32[120,512]{1,0:T(8,128)}, f32[896,896]{1,0:T(8,128)}) custom-call(s32[1]{0:T(128)} %bitcast.first, s32[4]{0:T(128)} %iota_xor_fusion.quarter_at, f32[512,512]{1,0:T(8,128)} %pivots.1.inverse_ref, f32[120,512]{1,0:T(8,128)} %bitcast.19, f32[896,512]{1,0:T(8,128)} %all-gather.6.cloned.1.call-done.rows_hbm, f32[896,896]{1,0:T(8,128)} %bitcast.17, ...), custom_call_target="tpu_custom_call" | custom-call | flops 2147483648 | bytes 12582912 | tf_op jit(solution)/shard_map/updates/pallas_call | solution.py:274
  253.3 6.2 %place.1 = f32[896,896]{1,0:T(8,128)} custom-call(f32[64,136,128]{2,1,0:T(8,128)} %all-to-all-done.incoming_hbm, f32[896,896]{1,0:T(8,128)} %get-tuple-element.5.base_hbm), custom_call_target="tpu_custom_call" | custom-call | flops 536870912 | bytes 10485760 | tf_op jit(solution)/shard_map/place/pallas_call | solution.py:339
  259.6 43.7 %reduce-scatter.2.cloned.1.call-done = f32[224,896]{1,0:T(8,128)} async-done(((f32[896,896]{1,0:T(8,128)}), f32[224,896]{1,0:T(8,128)}) %reduce-scatter.2.cloned.1.call-update) | async-done | bytes 802832 | tf_op jit(solution)/shard_map/reduce_scatter | solution.py:439
  (27 shorter events, 0.2 us)
Async XLA Ops:
  7.2 38.7 %collective-permute-start = (f32[120,512]{1,0:T(8,128)}, f32[120,512]{1,0:T(8,128)S(1)}, u32[]{:S(2)}, u32[]{:S(2)}) collective-permute-start(f32[120,512]{1,0:T(8,128)} %bitcast.18), channel_id=1, source_target_pairs={{0,8},{1,9},{2,10},{3,11},{4,12},{64,72},{65,73},{66,74},{67,75},{... | collective-permute-start | bytes 737288 | tf_op jit(solution)/shard_map/ppermute | solution.py:391
  16.8 9.7 %copy-start.5 = (s32[1,2,3]{2,1,0:T(2,128)S(1)}, s32[1,2,3]{2,1,0:T(2,128)}, u32[]{:S(2)}) copy-start(s32[1,2,3]{2,1,0:T(2,128)} %param.10) | copy-start | bytes 76
  40.1 5.8 %copy-start.1 = (f32[1,120,512]{2,1,0:T(8,128)S(1)}, f32[1,120,512]{2,1,0:T(8,128)}, u32[]{:S(2)}) copy-start(f32[1,120,512]{2,1,0:T(8,128)} %param.14) | copy-start | bytes 737284
  40.1 213.3 %all-to-all-start = ((f32[64,136,128]{2,1,0:T(8,128)}), f32[64,136,128]{2,1,0:T(8,128)}, u32[]{:S(2)}, u32[]{:S(2)}) async-start(f32[64,136,128]{2,1,0:T(8,128)} %middles.1), calls=%async_computation | async-start | bytes 8912896 | tf_op jit(solution)/shard_map/all_to_all | solution.py:426
  45.8 35.7 %all-gather.8.cloned.1.call-start = ((), (), s32[]{:S(2)}) async-start(), calls=%async_computation.4 | async-start | bytes 1392640 | tf_op jit(solution)/shard_map/all_gather | solution.py:400
  46.7 163.3 %all-gather.10.cloned.1.call-start = ((), (), s32[]{:S(2)}) async-start(), calls=%async_computation.5 | async-start | bytes 2211840 | tf_op jit(solution)/shard_map/all_gather | solution.py:403
  83.1 151.8 %all-gather.6.cloned.1.call-start = ((), (), s32[]{:S(2)}) async-start(), calls=%async_computation.2 | async-start | bytes 2064384 | tf_op jit(solution)/shard_map/all_gather | solution.py:427
  83.2 78.6 %collective-permute-start.1 = (f32[120,512]{1,0:T(8,128)S(1)}, f32[120,512]{1,0:T(8,128)S(1)}, u32[]{:S(2)}, u32[]{:S(2)}) collective-permute-start(f32[120,512]{1,0:T(8,128)S(1)} %bitcast.20), channel_id=1, source_target_pairs={{4,0},{5,1},{6,2},{7,3},{8,4},{9,6},{10,7},{11,8},{12,9},{13,10},{... | collective-permute-start | bytes 737288 | tf_op jit(solution)/shard_map/ppermute | solution.py:392
  84.5 95.0 %collective-permute-start.3 = (f32[120,512]{1,0:T(8,128)S(1)}, f32[120,512]{1,0:T(8,128)S(1)}, u32[]{:S(2)}, u32[]{:S(2)}) collective-permute-start(f32[120,512]{1,0:T(8,128)S(1)} %bitcast.21), channel_id=1, source_target_pairs={{5,0},{6,1},{7,2},{9,5},{10,6},{11,7},{12,8},{13,9},{14,10},{15,11... | collective-permute-start | bytes 737288 | tf_op jit(solution)/shard_map/ppermute | solution.py:393
  85.8 76.0 %collective-permute-start.2 = (f32[8,512]{1,0:T(8,128)S(1)}, f32[8,512]{1,0:T(8,128)S(1)}, u32[]{:S(2)}, u32[]{:S(2)}) collective-permute-start(f32[8,512]{1,0:T(8,128)S(1)} %slice_bitcast_fusion), channel_id=1, source_target_pairs={{8,5},{22,20},{36,35},{50,50},{72,69},{86,84},{100,99},{114,114},{... | collective-permute-start | bytes 49160 | tf_op jit(solution)/shard_map/ppermute | solution.py:394
  180.3 123.0 %reduce-scatter.2.cloned.1.call-start = ((), (), s32[]{:S(2)}) async-start(), calls=%async_computation.3 | async-start | bytes 4014080 | tf_op jit(solution)/shard_map/reduce_scatter | solution.py:439
  180.3 16.8 %collective-permute-start.4 = (f32[112,512]{1,0:T(8,128)}, f32[112,512]{1,0:T(8,128)S(1)}, u32[]{:S(2)}, u32[]{:S(2)}) collective-permute-start(f32[112,512]{1,0:T(8,128)} %fusion.1), channel_id=1, source_target_pairs={{0,0},{1,8},{2,16},{3,24},{4,32},{5,40},{6,48},{7,56},{8,1},{9,9},... | collective-permute-start | bytes 688136 | tf_op jit(solution)/shard_map/ppermute | solution.py:404
  187.8 10.8 %collective-permute-start.5 = (f32[112,512]{1,0:T(8,128)}, f32[112,512]{1,0:T(8,128)S(1)}, u32[]{:S(2)}, u32[]{:S(2)}) collective-permute-start(f32[112,512]{1,0:T(8,128)} %fusion.1), channel_id=1, source_target_pairs={{0,8},{1,0},{2,24},{3,16},{4,40},{5,32},{6,56},{7,48},{8,9},{9,1},... | collective-permute-start | bytes 688136 | tf_op jit(solution)/shard_map/ppermute | solution.py:407
  198.7 36.2 %copy-start = (f32[224,512]{1,0:T(8,128)}, f32[224,512]{1,0:T(8,128)S(1)}, u32[]{:S(2)}) copy-start(f32[224,512]{1,0:T(8,128)S(1)} %maximum_select_fusion.rest_0_) | copy-start | bytes 1376260
  198.7 36.2 %collective-permute-start.8 = (f32[224,512]{1,0:T(8,128)S(1)}, f32[224,512]{1,0:T(8,128)S(1)}, u32[]{:S(2)}, u32[]{:S(2)}) collective-permute-start(f32[224,512]{1,0:T(8,128)S(1)} %maximum_select_fusion.rest_0_), channel_id=1, source_target_pairs={{0,48},{1,49},{2,50},{3,51},{4,52},{5,53},{6,54},{7,55},{8,56},{9,... | collective-permute-start | bytes 1376264 | tf_op jit(solution)/shard_map/ppermute | solution.py:424
  207.0 27.9 %collective-permute-start.7 = (f32[224,512]{1,0:T(8,128)S(1)}, f32[224,512]{1,0:T(8,128)S(1)}, u32[]{:S(2)}, u32[]{:S(2)}) collective-permute-start(f32[224,512]{1,0:T(8,128)S(1)} %maximum_select_fusion.rest_0_), channel_id=1, source_target_pairs={{0,32},{1,33},{2,34},{3,35},{4,36},{5,37},{6,38},{7,39},{8,40},{9,... | collective-permute-start | bytes 1376264 | tf_op jit(solution)/shard_map/ppermute | solution.py:424
  209.4 25.5 %collective-permute-start.6 = (f32[224,512]{1,0:T(8,128)S(1)}, f32[224,512]{1,0:T(8,128)S(1)}, u32[]{:S(2)}, u32[]{:S(2)}) collective-permute-start(f32[224,512]{1,0:T(8,128)S(1)} %maximum_select_fusion.rest_0_), channel_id=1, source_target_pairs={{0,16},{1,17},{2,18},{3,19},{4,20},{5,21},{6,22},{7,23},{8,24},{9,... | collective-permute-start | bytes 1376264 | tf_op jit(solution)/shard_map/ppermute | solution.py:424
  234.9 0.8 copy-start.2
  234.9 0.9 copy-start.3
  234.9 1.0 copy-start.4
Sparse Core Ops, SparseCore 0:
  48.9 32.4 all-gather.7
  83.8 82.4 all-gather.9
  180.4 42.3 all-gather.5
  259.7 43.5 reduce-scatter.1
